TPU v7x, 16 devices: a 4x2x1 block of a 4x4x8 slice. The times are simulated.
16 devices in a mesh: dp: 2 (over y, z), tp: 8 (over x, core).
Axes of the slice: x: 4, y: 2, z: 1, core: 2. Of those that a mesh axis runs over, the one named last changes fastest.
The devices are a block of a 4x4x8 slice.
Arguments:
- x_in: bfloat16 [32, 512, 2560], P('dp', 'tp'), parts along dimension 0
- rope_angle: float32 [512, 16], replicated
- ln_gain: float32 [2560], replicated
- ln_bias: float32 [2560], replicated
- w_q: bfloat16 [2560, 2560], P(None, 'tp')
- b_q: float32 [32, 80], P('tp')
- w_k: bfloat16 [2560, 2560], P(None, 'tp')
- b_k: float32 [32, 80], P('tp')
- w_v: bfloat16 [2560, 2560], P(None, 'tp')
- b_v: float32 [32, 80], P('tp')
- w_o: bfloat16 [2560, 2560], P('tp')
- b_o: float32 [2560], replicated
- w_up: bfloat16 [2560, 10240], P(None, 'tp')
- b_up: float32 [10240], P('tp')
- w_down: bfloat16 [10240, 2560], P('tp')
- b_down: float32 [2560], replicated
- dy_out: bfloat16 [32, 512, 2560], P('dp', 'tp'), parts along dimension 0
Outputs:
- output 1: bfloat16 [32, 512, 2560], P('dp', 'tp'), parts along dimension 0
- output 2: float32 [32, 512, 2560], P('dp', 'tp'), parts along dimension 0
- output 3: float32 [5120], P('dp'), parts along dimension 0
- output 4: float32 [5120], P('dp'), parts along dimension 0
- output 5: float32 [5120, 2560], P('dp', 'tp'), parts along dimension 0
- output 6: float32 [64, 80], P(('dp', 'tp')), parts along dimension 0
- output 7: float32 [5120, 2560], P('dp', 'tp'), parts along dimension 0
- output 8: float32 [64, 80], P(('dp', 'tp')), parts along dimension 0
- output 9: float32 [5120, 2560], P('dp', 'tp'), parts along dimension 0
- output 10: float32 [64, 80], P(('dp', 'tp')), parts along dimension 0
- output 11: float32 [5120, 2560], P(('dp', 'tp')), parts along dimension 0
- output 12: float32 [5120], P('dp'), parts along dimension 0
- output 13: float32 [5120, 10240], P('dp', 'tp'), parts along dimension 0
- output 14: float32 [20480], P(('dp', 'tp')), parts along dimension 0
- output 15: float32 [20480, 2560], P(('dp', 'tp')), parts along dimension 0
- output 16: float32 [5120], P('dp'), parts along dimension 0
There are 2 independent parts. A program takes and returns all parts, laid end to end along the dimension named above; an argument that names none is the same for every part.
All inputs are finite; a program needn't handle non-finite values.
Results may differ from a plain program's by a relative error of at most 0.02.
Values are sent between devices in bfloat16 or wider.
A program may use at most 768 MiB of HBM per device.

v0:
```python
import jax
import jax.numpy as jnp
from jax import lax
from jax.sharding import PartitionSpec as P, NamedSharding

LN_EPS = 1e-5


def norm_stats(x_blk):
    x_f = x_blk.astype(jnp.float32)
    centered = x_f - jnp.mean(x_f, axis=-1, keepdims=True)
    inv_std = lax.rsqrt(jnp.mean(centered * centered, axis=-1, keepdims=True) + LN_EPS)
    return centered * inv_std, inv_std


def norm_backward(d_h, normed, inv_std, ln_gain):
    d_norm = d_h * ln_gain
    return inv_std * (d_norm - jnp.mean(d_norm, axis=-1, keepdims=True)
                      - normed * jnp.mean(d_norm * normed, axis=-1, keepdims=True))


def gelu_tanh(t):
    return jax.nn.gelu(t, approximate=True)


def rope_tables(rope_angle):
    angle_pair = jnp.concatenate([rope_angle, rope_angle], axis=-1)[:, None, :]
    return jnp.cos(angle_pair), jnp.sin(angle_pair)


def rope_apply(t, cos_t, sin_t):
    rot_dim = cos_t.shape[-1]
    half_rot = rot_dim // 2
    t_rot = t[..., :rot_dim].astype(jnp.float32)
    turned = jnp.concatenate([-t_rot[..., half_rot:], t_rot[..., :half_rot]], axis=-1)
    return jnp.concatenate([t_rot * cos_t + turned * sin_t, t[..., rot_dim:].astype(jnp.float32)], axis=-1)


def causal_mask(q_len, k_len, q_start):
    return (q_start + jnp.arange(q_len))[:, None] >= jnp.arange(k_len)[None, :]


def attn_forward(q_r, k_r, v_p, causal):
    attn_scale = q_r.shape[-1] ** -0.5
    scores = jnp.einsum('bqhd,bkhd->bhqk', q_r, k_r, preferred_element_type=jnp.float32) * attn_scale
    prob_f = jax.nn.softmax(jnp.where(causal, scores, -1e30), axis=-1)
    prob_bf = prob_f.astype(jnp.bfloat16)
    context = jnp.einsum('bhqk,bkhd->bqhd', prob_bf, v_p, preferred_element_type=jnp.float32)
    return context.astype(jnp.bfloat16), prob_f, prob_bf


def attn_backward(d_ctx, q_r, k_r, v_p, prob_f, prob_bf):
    attn_scale = q_r.shape[-1] ** -0.5
    d_prob = jnp.einsum('bqhd,bkhd->bhqk', d_ctx, v_p, preferred_element_type=jnp.float32)
    d_v = jnp.einsum('bhqk,bqhd->bkhd', prob_bf, d_ctx, preferred_element_type=jnp.float32)
    d_score = (prob_f * (d_prob - jnp.sum(d_prob * prob_f, axis=-1, keepdims=True)) * attn_scale).astype(jnp.bfloat16)
    d_q = jnp.einsum('bhqk,bkhd->bqhd', d_score, k_r, preferred_element_type=jnp.float32)
    d_k = jnp.einsum('bhqk,bqhd->bkhd', d_score, q_r, preferred_element_type=jnp.float32)
    return d_q, d_k, d_v


def layer_body(x_blk, rope_angle, ln_gain, ln_bias, w_q, b_q, w_k, b_k, w_v, b_v, w_o, b_o, w_up, b_up, w_down, b_down, dy_blk):
    normed, inv_std = norm_stats(x_blk)
    h_loc = (normed * ln_gain + ln_bias).astype(jnp.bfloat16)
    h_full = lax.all_gather(h_loc, 'tp', axis=1, tiled=True)
    n_seq, seq_len, model_dim = h_full.shape
    heads_loc, head_dim = b_q.shape
    cos_t, sin_t = rope_tables(rope_angle)

    def project(w_mat, b_vec):
        linear = jnp.einsum('bsd,de->bse', h_full, w_mat, preferred_element_type=jnp.float32)
        return (linear.reshape(n_seq, seq_len, heads_loc, head_dim) + b_vec).astype(jnp.bfloat16)

    q_r = rope_apply(project(w_q, b_q), cos_t, sin_t).astype(jnp.bfloat16)
    k_r = rope_apply(project(w_k, b_k), cos_t, sin_t).astype(jnp.bfloat16)
    v_p = project(w_v, b_v)
    context, prob_f, prob_bf = attn_forward(q_r, k_r, v_p, causal_mask(seq_len, seq_len, 0))
    ctx_flat = context.reshape(n_seq, seq_len, heads_loc * head_dim)
    act_f, gelu_pull = jax.vjp(gelu_tanh, jnp.einsum('bsd,df->bsf', h_full, w_up, preferred_element_type=jnp.float32) + b_up)
    act_bf = act_f.astype(jnp.bfloat16)
    branch = (jnp.einsum('bsc,ce->bse', ctx_flat, w_o, preferred_element_type=jnp.float32)
              + jnp.einsum('bsf,fe->bse', act_bf, w_down, preferred_element_type=jnp.float32))
    branch_sum = lax.psum_scatter(branch.astype(jnp.bfloat16), 'tp', scatter_dimension=1, tiled=True)
    y_blk = (x_blk.astype(jnp.float32) + branch_sum.astype(jnp.float32) + b_o + b_down).astype(jnp.bfloat16)

    dy_f = dy_blk.astype(jnp.float32)
    dy_full = lax.all_gather(dy_blk, 'tp', axis=1, tiled=True)
    grad_wdown = jnp.einsum('bsf,bse->fe', act_bf, dy_full, preferred_element_type=jnp.float32)
    d_pre = gelu_pull(jnp.einsum('bse,fe->bsf', dy_full, w_down, preferred_element_type=jnp.float32))[0]
    grad_bup = jnp.sum(d_pre, axis=(0, 1))
    d_pre_bf = d_pre.astype(jnp.bfloat16)
    grad_wup = jnp.einsum('bsd,bsf->df', h_full, d_pre_bf, preferred_element_type=jnp.float32)
    d_h = jnp.einsum('bsf,df->bsd', d_pre_bf, w_up, preferred_element_type=jnp.float32)
    grad_wo = jnp.einsum('bsc,bse->ce', ctx_flat, dy_full, preferred_element_type=jnp.float32)
    d_ctx = jnp.einsum('bse,ce->bsc', dy_full, w_o, preferred_element_type=jnp.float32).astype(jnp.bfloat16)
    d_qr, d_kr, d_v = attn_backward(d_ctx.reshape(n_seq, seq_len, heads_loc, head_dim), q_r, k_r, v_p, prob_f, prob_bf)
    proj_grads = []
    for d_proj, w_mat in ((rope_apply(d_qr, cos_t, -sin_t), w_q), (rope_apply(d_kr, cos_t, -sin_t), w_k), (d_v, w_v)):
        d_bf = d_proj.astype(jnp.bfloat16).reshape(n_seq, seq_len, heads_loc * head_dim)
        proj_grads.append(jnp.einsum('bsd,bsc->dc', h_full, d_bf, preferred_element_type=jnp.float32))
        proj_grads.append(jnp.sum(d_proj, axis=(0, 1)))
        d_h = d_h + jnp.einsum('bsc,dc->bsd', d_bf, w_mat, preferred_element_type=jnp.float32)
    d_h_loc = lax.psum_scatter(d_h.astype(jnp.bfloat16), 'tp', scatter_dimension=1, tiled=True).astype(jnp.float32)
    small_sums = lax.psum(jnp.stack([jnp.sum(d_h_loc * normed, axis=(0, 1)), jnp.sum(d_h_loc, axis=(0, 1)),
                                     jnp.sum(dy_f, axis=(0, 1))]), 'tp')
    d_x = dy_f + norm_backward(d_h_loc, normed, inv_std, ln_gain)
    return (y_blk, d_x, small_sums[0], small_sums[1], proj_grads[0], proj_grads[1], proj_grads[2], proj_grads[3],
            proj_grads[4], proj_grads[5], grad_wo, small_sums[2], grad_wup, grad_bup, grad_wdown, small_sums[2])


def solution(mesh):
    row_spec = P('dp', 'tp', None)
    col_spec = P(None, 'tp')
    head_spec = P('tp', None)
    grad_cols = P('dp', 'tp')
    grad_rows = P(('dp', 'tp'), None)
    in_specs = (row_spec, P(None, None), P(None), P(None), col_spec, head_spec, col_spec, head_spec,
                col_spec, head_spec, P('tp', None), P(None), col_spec, P('tp'), P('tp', None), P(None), row_spec)
    out_specs = (row_spec, row_spec, P('dp'), P('dp'), grad_cols, grad_rows, grad_cols, grad_rows, grad_cols,
                 grad_rows, grad_rows, P('dp'), grad_cols, P(('dp', 'tp')), grad_rows, P('dp'))
    return jax.shard_map(layer_body, mesh=mesh, in_specs=in_specs, out_specs=out_specs, check_vma=False)
```

profile of v0, /device:TPU:112, one launch (start us, length us, event | category | flops | bytes accessed | tf_op | source)
XLA Modules:
  0.0 1538.3 jit_solution(3033722720317955987)
XLA Ops:
  7.3 3.4 convert_reduce_fusion.1
  10.7 4.0 fusion.36
  14.8 0.6 copy-done.18
  15.4 4.3 fusion.33
  19.9 0.7 all-gather.5.cloned.1.call-update
  20.6 0.5 reduce-scatter.5.cloned.1.call-start
  21.2 0.2 fusion.99
  21.5 0.6 neg.25
  22.1 0.8 iota_compare_fusion
  22.9 188.8 %all-gather.3.cloned.1.call-done = bf16[16,512,2560]{2,1,0:T(8,128)(2,1)} async-done(((bf16[16,64,2560]{2,1,0:T(8,128)(2,1)}), bf16[16,512,2560]{2,1,0:T(8,128)(2,1)}) %all-gather.3.cloned.1.call-update) | async-done | bytes 41943056 | tf_op jit(solution)/shard_map/all_gather | solution.py:65
  211.7 25.6 %fusion.76 = f32[16,512,320]{1,2,0:T(8,128)} fusion(bf16[16,512,2560]{2,1,0:T(8,128)(2,1)} %all-gather.3.cloned.1.call-done, bf16[2560,320]{0,1:T(8,128)(2,1)S(1)} %copy-done.6), kind=kOutput, calls=%fused_computation.109 | convolution fusion | flops 13421772800 | bytes 54067200 | tf_op jit(solution)/shard_map/bsd,de->bse/dot_general | solution.py:71
  237.3 25.6 %fusion.80 = f32[16,512,320]{1,2,0:T(8,128)} fusion(bf16[16,512,2560]{2,1,0:T(8,128)(2,1)} %all-gather.3.cloned.1.call-done, bf16[2560,320]{0,1:T(8,128)(2,1)S(1)} %copy-done), kind=kOutput, calls=%fused_computation.113 | convolution fusion | flops 13421772800 | bytes 54067200 | tf_op jit(solution)/shard_map/bsd,de->bse/dot_general | solution.py:71
  263.0 8.6 add_convert_fusion.2
  271.5 2.0 slice.88
  273.5 2.0 slice.84
  275.5 0.6 slice_convert_fusion
  276.1 0.6 slice_convert_fusion.1
  276.7 0.9 slice_negate_fusion.2
  277.6 0.5 slice_negate_fusion.3
  278.1 3.2 fusion.58
  281.3 36.6 %fusion.100 = (f32[16,4,512]{2,1,0:T(4,128)S(1)}, f32[16,4,512,512]{2,3,1,0:T(8,128)}) fusion(pred[512,512]{0,1:T(8,128)(4,1)} %iota_compare_fusion, bf16[16,512,4,48]{1,3,2,0:T(8,128)(2,1)} %slice.88, bf16[16,512,4,32]{1,3,2,0:T(8,128)(2,1)} %get-tuple-element.37, bf16[16,512,4,48]{1,3,2,0:T(8,128)(2,1)} %slice.84, ...), kind=kOutput, calls=%fused_computation.142 | convolution fusion | flops 2772435456 | bytes 77987840 | tf_op jit(solution)/shard_map/sub | solution.py:46
  317.9 83.8 %all-gather.5.cloned.1.call-done = bf16[16,512,2560]{2,1,0:T(8,128)(2,1)} async-done(((bf16[16,64,2560]{2,1,0:T(8,128)(2,1)}), bf16[16,512,2560]{2,1,0:T(8,128)(2,1)}) %all-gather.5.cloned.1.call-update) | async-done | bytes 41943056 | tf_op jit(solution)/shard_map/all_gather | solution.py:87
  401.7 24.3 %convolution_convert_fusion = bf16[16,512,320]{1,2,0:T(8,128)(2,1)} fusion(bf16[16,512,2560]{2,1,0:T(8,128)(2,1)} %all-gather.5.cloned.1.call-done, bf16[320,2560]{1,0:T(8,128)(2,1)S(1)} %copy-done.10), kind=kOutput, calls=%fused_computation.96 | convolution fusion | flops 13424394240 | bytes 48824320 | tf_op jit(solution)/shard_map/bse,ce->bsc/dot_general | solution.py:95
  426.0 30.8 %bitcast_convert_fusion = (bf16[16,512,4,80]{1,3,2,0:T(8,128)(2,1)}, f32[16,4,80,512]{3,2,1,0:T(8,128)}) fusion(bf16[16,512,4,80]{1,3,2,0:T(8,128)(2,1)} %bitcast.100, f32[16,4,512,512]{2,3,1,0:T(8,128)} %get-tuple-element.41, f32[16,4,512]{2,1,0:T(4,128)S(1)} %get-tuple-element.40), kind=kOutput, calls=%fused_computation.59 | convolution fusion | flops 2720530432 | bytes 88211456 | tf_op jit(solution)/shard_map/bhqk,bqhd->bkhd/dot_general | solution.py:55
  456.9 25.8 %fusion.84 = f32[16,512,320]{1,2,0:T(8,128)} fusion(bf16[16,512,2560]{2,1,0:T(8,128)(2,1)} %all-gather.3.cloned.1.call-done, bf16[2560,320]{0,1:T(8,128)(2,1)S(1)} %copy-done.8), kind=kOutput, calls=%fused_computation.117 | convolution fusion | flops 13421772800 | bytes 54067200 | tf_op jit(solution)/shard_map/bsd,de->bse/dot_general | solution.py:71
  482.7 28.4 %fusion.70 = f32[16,4,512,512]{2,3,1,0:T(8,128)} fusion(bf16[16,512,4,80]{1,3,2,0:T(8,128)(2,1)} %bitcast.101, f32[16,512,4,80]{1,3,2,0:T(8,128)} %bitcast.96, f32[4,80]{1,0:T(4,128)S(1)} %copy-done.23), kind=kOutput, calls=%fused_computation.103 | convolution fusion | flops 2689597440 | bytes 82838784 | tf_op jit(solution)/shard_map/bqhd,bkhd->bhqk/dot_general | solution.py:54
  511.1 86.8 %fusion.61 = f32[16,512,4,80]{1,3,2,0:T(8,128)} fusion(f32[16,4,512,512]{2,3,1,0:T(8,128)} %fusion.70, bf16[16,512,4,48]{1,3,2,0:T(8,128)(2,1)} %slice.88, bf16[16,512,4,32]{1,3,2,0:T(8,128)(2,1)} %get-tuple-element.37, f32[16,4,512,512]{2,3,1,0:T(8,128)} %get-tuple-element.41, f32[16,4,512]{2,1,0:T(4,128)S(1)} %get-tuple-element.40), kind=kOutput, calls=%fused_computation.93 | convolution fusion | flops 2812314112 | bytes 150077440 | tf_op jit(solution)/shard_map/bhqk,bkhd->bqhd/dot_general | solution.py:57
  597.9 86.9 %fusion.64 = f32[16,512,4,80]{1,3,2,0:T(8,128)} fusion(f32[16,4,512,512]{2,3,1,0:T(8,128)} %fusion.70, bf16[16,512,4,48]{1,3,2,0:T(8,128)(2,1)} %slice.84, bf16[16,512,4,32]{1,3,2,0:T(8,128)(2,1)} %get-tuple-element.36, f32[16,4,512,512]{2,3,1,0:T(8,128)} %get-tuple-element.41, f32[16,4,512]{2,1,0:T(4,128)S(1)} %get-tuple-element.40), kind=kOutput, calls=%fused_computation.94 | convolution fusion | flops 2812314112 | bytes 150077440 | tf_op jit(solution)/shard_map/bhqk,bqhd->bkhd/dot_general | solution.py:58
  684.8 3.3 slice_negate_fusion
  688.2 7.2 slice.96
  695.4 0.9 slice_negate_fusion.1
  696.3 3.9 slice.92
  700.2 5.2 fusion.56
  705.4 8.7 fusion.47
  714.1 34.3 %fusion.78 = f32[16,512,2560]{2,1,0:T(8,128)} fusion(bf16[16,512,320]{1,2,0:T(8,128)(2,1)} %bitcast.90, bf16[2560,320]{0,1:T(8,128)(2,1)S(1)} %copy-done), kind=kOutput, calls=%fused_computation.111 | convolution fusion | flops 13421772800 | bytes 90767360 | tf_op jit(solution)/shard_map/bsc,dc->bsd/dot_general | solution.py:102
  748.4 6.1 fusion.45
  754.5 34.2 %fusion.74 = f32[16,512,2560]{2,1,0:T(8,128)} fusion(bf16[16,512,320]{1,2,0:T(8,128)(2,1)} %bitcast.92, bf16[2560,320]{0,1:T(8,128)(2,1)S(1)} %copy-done.7), kind=kOutput, calls=%fused_computation.107 | convolution fusion | flops 13421772800 | bytes 90767360 | tf_op jit(solution)/shard_map/bsc,dc->bsd/dot_general | solution.py:102
  788.7 34.4 %fusion.82 = f32[16,512,2560]{2,1,0:T(8,128)} fusion(bf16[16,512,320]{1,2,0:T(8,128)(2,1)} %bitcast.102, bf16[2560,320]{0,1:T(8,128)(2,1)S(1)} %copy-done.9), kind=kOutput, calls=%fused_computation.115 | convolution fusion | flops 13421772800 | bytes 90767360 | tf_op jit(solution)/shard_map/bsc,dc->bsd/dot_general | solution.py:102
  823.2 60.5 %fusion.53 = f32[16,512,1280]{2,1,0:T(8,128)} fusion(bf16[16,512,2560]{2,1,0:T(8,128)(2,1)} %all-gather.3.cloned.1.call-done, bf16[2560,1280]{1,0:T(8,128)(2,1)S(1)} %bitcast.107), kind=kOutput, calls=%fused_computation.73 | convolution fusion | flops 53687091200 | bytes 90439680 | tf_op jit(solution)/shard_map/bsd,df->bsf/dot_general | solution.py:79
  883.7 85.5 %fusion.101 = (f32[1280]{0:T(1024)}, bf16[16,512,1280]{2,1,0:T(8,128)(2,1)}) fusion(f32[16,512,1280]{2,1,0:T(8,128)} %fusion.53, f32[1280]{0:T(1024)S(1)} %copy-done.30, bf16[16,512,2560]{2,1,0:T(8,128)(2,1)} %all-gather.5.cloned.1.call-done, bf16[1280,2560]{1,0:T(8,128)(2,1)} %param.31), kind=kOutput, calls=%fused_computation.143 | convolution fusion | flops 53917777920 | bytes 111421440 | tf_op jit(solution)/shard_map/bse,fe->bsf/dot_general | solution.py:89
  969.2 106.7 %add_convert_fusion = bf16[16,512,2560]{2,1,0:T(8,128)(2,1)} fusion(f32[16,512,2560]{2,1,0:T(8,128)} %fusion.82, f32[16,512,2560]{2,1,0:T(8,128)} %fusion.74, f32[16,512,2560]{2,1,0:T(8,128)} %fusion.78, bf16[16,512,1280]{2,1,0:T(8,128)(2,1)} %get-tuple-element.45, bf16[2560,1280]{1,0:T(8,128)(2,1)} %param.29), kind=kOutput, calls=%fused_computation.2 | convolution fusion | flops 53770977280 | bytes 321126400 | tf_op jit(solution)/shard_map/bsf,df->bsd/dot_general | solution.py:93
  1076.0 0.1 reduce-scatter.3.cloned.1.call-start
  1076.0 0.5 copy-done.24
  1076.6 0.2 copy-done.34
  1076.8 27.7 %fusion.67 = bf16[16,4,80,512]{3,2,1,0:T(8,128)(2,1)} fusion(f32[16,512,4,80]{1,3,2,0:T(8,128)} %bitcast.97, f32[4,80]{1,0:T(4,128)S(1)} %copy-done.24, f32[16,4,512,512]{2,3,1,0:T(8,128)} %get-tuple-element.41, f32[16,4,512]{2,1,0:T(4,128)S(1)} %copy-done.34), kind=kOutput, calls=%fused_computation.95 | convolution fusion | flops 2725773312 | bytes 82969856 | tf_op jit(solution)/shard_map/bhqk,bkhd->bqhd/dot_general | solution.py:48
  1104.6 34.3 %fusion.72 = f32[16,512,2560]{2,1,0:T(8,128)} fusion(bf16[16,512,320]{1,2,0:T(8,128)(2,1)} %bitcast.104, bf16[320,2560]{1,0:T(8,128)(2,1)S(1)} %copy-done.11), kind=kOutput, calls=%fused_computation.105 | convolution fusion | flops 13421772800 | bytes 90767360 | tf_op jit(solution)/shard_map/bsc,ce->bse/dot_general | solution.py:81
  1138.9 71.2 %add_convert_fusion.1 = bf16[16,512,2560]{2,1,0:T(8,128)(2,1)} fusion(f32[16,512,2560]{2,1,0:T(8,128)} %fusion.72, bf16[1280,2560]{1,0:T(8,128)(2,1)} %param.31, f32[16,512,1280]{2,1,0:T(8,128)} %fusion.53, f32[1280]{0:T(1024)S(1)} %copy-done.31), kind=kOutput, calls=%fused_computation.3 | convolution fusion | flops 53833891840 | bytes 174330880 | tf_op jit(solution)/shard_map/bsf,fe->bse/dot_general | solution.py:82
  1210.1 5.3 fusion.46
  1215.4 0.4 copy-done.3
  1215.9 1.2 copy-done.5
  1217.1 1.2 fusion.44
  1218.3 5.1 bitcast_reduce_fusion
  1223.4 23.8 %convolution_bitcast_fusion.5 = f32[320,2560]{1,0:T(8,128)} fusion(bf16[16,512,320]{1,2,0:T(8,128)(2,1)} %bitcast.105, bf16[16,512,2560]{2,1,0:T(8,128)(2,1)} %all-gather.5.cloned.1.call-done), kind=kOutput, calls=%fused_computation.80 | convolution fusion | flops 13421772800 | bytes 50462720 | tf_op jit(solution)/shard_map/bsc,bse->ce/dot_general | solution.py:94
  1247.3 23.5 %convolution_bitcast_fusion.2 = f32[2560,320]{0,1:T(8,128)} fusion(bf16[16,512,320]{1,2,0:T(8,128)(2,1)} %bitcast.103, bf16[16,512,2560]{2,1,0:T(8,128)(2,1)} %all-gather.3.cloned.1.call-done), kind=kOutput, calls=%fused_computation.77 | convolution fusion | flops 13421772800 | bytes 50462720 | tf_op jit(solution)/shard_map/bsd,bsc->dc/dot_general | solution.py:100
  1270.8 23.7 %convolution_bitcast_fusion.3 = f32[2560,320]{0,1:T(8,128)} fusion(bf16[16,512,320]{1,2,0:T(8,128)(2,1)} %bitcast.93, bf16[16,512,2560]{2,1,0:T(8,128)(2,1)} %all-gather.3.cloned.1.call-done), kind=kOutput, calls=%fused_computation.78 | convolution fusion | flops 13421772800 | bytes 50462720 | tf_op jit(solution)/shard_map/bsd,bsc->dc/dot_general | solution.py:100
  1294.4 23.6 %convolution_bitcast_fusion.4 = f32[2560,320]{0,1:T(8,128)} fusion(bf16[16,512,320]{1,2,0:T(8,128)(2,1)} %bitcast.91, bf16[16,512,2560]{2,1,0:T(8,128)(2,1)} %all-gather.3.cloned.1.call-done), kind=kOutput, calls=%fused_computation.79 | convolution fusion | flops 13421772800 | bytes 50462720 | tf_op jit(solution)/shard_map/bsd,bsc->dc/dot_general | solution.py:100
  1318.0 63.8 %convolution_bitcast_fusion.1 = f32[2560,1280]{1,0:T(8,128)} fusion(bf16[16,512,2560]{2,1,0:T(8,128)(2,1)} %all-gather.3.cloned.1.call-done, bf16[16,512,1280]{2,1,0:T(8,128)(2,1)} %get-tuple-element.45), kind=kOutput, calls=%fused_computation.41 | convolution fusion | flops 53687091200 | bytes 76021760 | tf_op jit(solution)/shard_map/bsd,bsf->df/dot_general | solution.py:92
  1381.8 75.6 %convolution_bitcast_fusion = f32[1280,2560]{1,0:T(8,128)} fusion(bf16[16,512,2560]{2,1,0:T(8,128)(2,1)} %all-gather.5.cloned.1.call-done, f32[16,512,1280]{2,1,0:T(8,128)} %fusion.53, f32[1280]{0:T(1024)S(1)} %copy-done.32), kind=kOutput, calls=%fused_computation.40 | convolution fusion | flops 53791948800 | bytes 96998400 | tf_op jit(solution)/shard_map/bsf,bse->fe/dot_general | solution.py:88
  1457.5 7.3 fusion.41
  1464.8 24.4 %reduce-scatter.3.cloned.1.call-done = bf16[16,64,2560]{2,1,0:T(8,128)(2,1)} async-done(((bf16[16,512,2560]{2,1,0:T(8,128)(2,1)}), bf16[16,64,2560]{2,1,0:T(8,128)(2,1)}) %reduce-scatter.3.cloned.1.call-update) | async-done | bytes 5242896 | tf_op jit(solution)/shard_map/reduce_scatter | solution.py:83
  1489.2 16.9 %convert_reduce_fusion.2 = (f32[2560]{0:T(1024)S(1)}, f32[16,64,2560]{2,1,0:T(8,128)}, bf16[16,64,2560]{2,1,0:T(8,128)(2,1)}) fusion(bf16[16,64,2560]{2,1,0:T(8,128)(2,1)} %param.33, f32[16,64]{1,0:T(8,128)S(1)} %broadcast_multiply_fusion, f32[16,64]{1,0:T(8,128)S(1)} %copy-done.16, bf16[16,64,2560]{2,1,0:T(8,128)(2,1)} %param.17, ...), kind=kLoop, calls=%fused_computation.38 | loop fusion | flops 44561920 | bytes 36757504 | tf_op jit(solution)/shard_map/reduce_sum | solution.py:105
  1506.2 24.0 %psum.7 = f32[3,2560]{1,0:T(4,128)S(1)} all-reduce(f32[3,2560]{1,0:T(4,128)S(1)} %pad_maximum_fusion.16), channel_id=1, replica_groups=mesh['dp'=2,'tp'=8] {'tp'}, use_global_device_ids=true, to_apply=%region_12.13 | all-reduce | flops 7680 | bytes 61440 | tf_op jit(solution)/shard_map/psum | solution.py:104
  1530.2 0.7 slice_reduce_fusion
  1530.9 0.6 copy.45
  (93 shorter events, 0.6 us)
Async XLA Ops:
  7.2 230.2 %copy-start = (bf16[2560,320]{0,1:T(8,128)(2,1)S(1)}, bf16[2560,320]{0,1:T(8,128)(2,1)}, u32[]{:S(2)}) copy-start(bf16[2560,320]{0,1:T(8,128)(2,1)} %param.21) | copy-start | bytes 4915204
  7.2 8.2 copy-start.20
  7.2 8.2 copy-start.25
  7.2 204.5 %all-gather.3.cloned.1.call-start = ((), (), s32[]{:S(2)}) async-start(), calls=%async_computation.2 | async-start | bytes 47185920 | tf_op jit(solution)/shard_map/all_gather | solution.py:65
  7.3 8.1 copy-start.2
  10.7 4.0 copy-start.15
  14.8 0.6 copy-start.18
  15.4 5.8 copy-start.17
  15.4 196.3 %copy-start.6 = (bf16[2560,320]{0,1:T(8,128)(2,1)S(1)}, bf16[2560,320]{0,1:T(8,128)(2,1)}, u32[]{:S(2)}) copy-start(bf16[2560,320]{0,1:T(8,128)(2,1)} %param.23) | copy-start | bytes 4915204
  19.8 381.8 %all-gather.5.cloned.1.call-start = ((), (), s32[]{:S(2)}) async-start(), calls=%async_computation.4 | async-start | bytes 47185920 | tf_op jit(solution)/shard_map/all_gather | solution.py:87
  20.6 1436.8 %reduce-scatter.5.cloned.1.call-start = ((), (), s32[]{:S(2)}) async-start(), calls=%async_computation.5 | async-start | bytes 47185920 | tf_op jit(solution)/shard_map/reduce_scatter | solution.py:103
  21.4 256.6 %copy-start.12 = (f32[512,32]{0,1:T(8,128)}, f32[512,32]{0,1:T(8,128)S(1)}, u32[]{:S(2)}) copy-start(f32[512,32]{0,1:T(8,128)S(1)} %get-tuple-element.38) | copy-start | bytes 196612
  237.3 25.6 %copy-start.28 = (f32[4,80]{1,0:T(4,128)S(1)}, f32[4,80]{1,0:T(4,128)}, u32[]{:S(2)}) copy-start(f32[4,80]{1,0:T(4,128)} %param.24) | copy-start | bytes 3844
  237.3 25.6 %copy-start.29 = (f32[4,80]{1,0:T(4,128)S(1)}, f32[4,80]{1,0:T(4,128)}, u32[]{:S(2)}) copy-start(f32[4,80]{1,0:T(4,128)} %param.22) | copy-start | bytes 3844
  281.3 120.4 %copy-start.10 = (bf16[320,2560]{1,0:T(8,128)(2,1)S(1)}, bf16[320,2560]{1,0:T(8,128)(2,1)}, u32[]{:S(2)}) copy-start(bf16[320,2560]{1,0:T(8,128)(2,1)} %param.27) | copy-start | bytes 4915204
  317.9 280.0 %copy-start.33 = (f32[16,4,512]{2,1,0:T(4,128)}, f32[16,4,512]{2,1,0:T(4,128)S(1)}, u32[]{:S(2)}) copy-start(f32[16,4,512]{2,1,0:T(4,128)S(1)} %get-tuple-element.40) | copy-start | bytes 393220
  426.0 30.8 %copy-start.8 = (bf16[2560,320]{0,1:T(8,128)(2,1)S(1)}, bf16[2560,320]{0,1:T(8,128)(2,1)}, u32[]{:S(2)}) copy-start(bf16[2560,320]{0,1:T(8,128)(2,1)} %param.25) | copy-start | bytes 4915204
  456.9 25.8 %copy-start.23 = (f32[4,80]{1,0:T(4,128)S(1)}, f32[4,80]{1,0:T(4,128)}, u32[]{:S(2)}) copy-start(f32[4,80]{1,0:T(4,128)} %param.26) | copy-start | bytes 3844
  684.8 10.5 slice-start
  684.8 10.5 slice-start.1
  688.1 7.2 slice-start.2
  695.4 4.8 copy-start.13
  695.4 4.8 copy-start.14
  705.4 43.0 %copy-start.4 = (f32[16,512,4,32]{1,3,2,0:T(8,128)}, f32[16,512,4,32]{1,3,2,0:T(8,128)S(1)}, u32[]{:S(2)}) copy-start(f32[16,512,4,32]{1,3,2,0:T(8,128)S(1)} %get-tuple-element.35) | copy-start | bytes 12582916
  748.4 6.1 copy-start.7
  754.5 34.2 %copy-start.9 = (bf16[2560,320]{0,1:T(8,128)(2,1)S(1)}, bf16[2560,320]{0,1:T(8,128)(2,1)}, u32[]{:S(2)}) copy-start(bf16[2560,320]{0,1:T(8,128)(2,1)} %param.25) | copy-start | bytes 4915204
  754.5 68.6 %slice-start.3 = ((s8[6553600]{0:T(1024)(128)(4,1)}), s8[4194304]{0:T(1024)(128)(4,1)S(1)}, s32[]{:S(2)}) async-start(s8[6553600]{0:T(1024)(128)(4,1)} %bitcast.106), calls=%async_computation.9 | async-start | bytes 8388608
  788.7 34.5 %slice-start.4 = ((s8[6553600]{0:T(1024)(128)(4,1)}), s8[2359296]{0:T(1024)(128)(4,1)S(1)}, s32[]{:S(2)}) async-start(s8[6553600]{0:T(1024)(128)(4,1)} %bitcast.106), calls=%async_computation.10 | async-start | bytes 4718592
  823.2 60.5 %copy-start.30 = (f32[1280]{0:T(1024)S(1)}, f32[1280]{0:T(1024)}, u32[]{:S(2)}) copy-start(f32[1280]{0:T(1024)} %param.30) | copy-start | bytes 15364
  1075.9 0.7 copy-start.24
  1075.9 0.9 copy-start.34
  1076.0 28.6 %copy-start.11 = (bf16[320,2560]{1,0:T(8,128)(2,1)S(1)}, bf16[320,2560]{1,0:T(8,128)(2,1)}, u32[]{:S(2)}) copy-start(bf16[320,2560]{1,0:T(8,128)(2,1)} %param.27) | copy-start | bytes 4915204
  1076.0 413.2 %reduce-scatter.3.cloned.1.call-start = ((), (), s32[]{:S(2)}) async-start(), calls=%async_computation.3 | async-start | bytes 47185920 | tf_op jit(solution)/shard_map/reduce_scatter | solution.py:83
  1104.6 34.3 %copy-start.31 = (f32[1280]{0:T(1024)S(1)}, f32[1280]{0:T(1024)}, u32[]{:S(2)}) copy-start(f32[1280]{0:T(1024)} %param.30) | copy-start | bytes 15364
  1210.1 5.8 copy-start.3
  1210.1 7.0 copy-start.5
  1318.0 63.8 %copy-start.32 = (f32[1280]{0:T(1024)S(1)}, f32[1280]{0:T(1024)}, u32[]{:S(2)}) copy-start(f32[1280]{0:T(1024)} %param.30) | copy-start | bytes 15364
  1381.8 75.6 %copy-start.16 = (f32[16,64]{1,0:T(8,128)S(1)}, f32[16,64]{1,0:T(8,128)}, u32[]{:S(2)}) copy-start(f32[16,64]{1,0:T(8,128)} %copy-done.15) | copy-start | bytes 12292
  1381.8 75.6 %copy-start.19 = (f32[16,64]{1,0:T(8,128)S(1)}, f32[16,64]{1,0:T(8,128)}, u32[]{:S(2)}) copy-start(f32[16,64]{1,0:T(8,128)} %copy-done.18) | copy-start | bytes 12292
  1381.8 75.6 %copy-start.21 = (f32[2560]{0:T(1024)S(1)}, f32[2560]{0:T(1024)}, u32[]{:S(2)}) copy-start(f32[2560]{0:T(1024)} %param.19) | copy-start | bytes 30724
  1457.4 31.8 %copy-start.26 = (f32[2560]{0:T(1024)S(1)}, f32[2560]{0:T(1024)}, u32[]{:S(2)}) copy-start(f32[2560]{0:T(1024)} %param.32) | copy-start | bytes 30724
  1457.4 31.8 %copy-start.27 = (f32[2560]{0:T(1024)S(1)}, f32[2560]{0:T(1024)}, u32[]{:S(2)}) copy-start(f32[2560]{0:T(1024)} %param.28) | copy-start | bytes 30724
  1464.8 66.7 %copy-start.1 = (bf16[2560,320]{0,1:T(8,128)(2,1)S(1)}, bf16[2560,320]{0,1:T(8,128)(2,1)}, u32[]{:S(2)}) copy-start(bf16[2560,320]{0,1:T(8,128)(2,1)} %param.21) | copy-start | bytes 4915204
  1530.9 0.6 copy-start.22
Sparse Core Ops, SparseCore 0:
  19.9 191.7 all-gather.2
  213.3 188.3 all-gather.4
  1076.1 205.2 reduce-scatter.4
  1283.6 205.5 reduce-scatter.2
where the time goes:
time: 1540 us
  matrix products  1090 us (71%)
  waiting for transfers between devices  298 us (19%)
  other arithmetic  87.6 us (6%)
  blocking collectives  24 us (2%)
  local copies, waits for them, and re-layouts  19.8 us (1%)
    all_gather x1, waiting for transfers between devices, layer_body(): h_full = lax.all_gather(h_loc, 'tp', axis=1, tiled=True)  189 us
    dot_general x1, matrix products, layer_body(): jnp.einsum('bsf,df->bsd', d_pre_bf, w_up, preferred_element_type=jnp.floa...  107 us
    dot_general x3, matrix products, layer_body(): jnp.einsum('bsc,dc->bsd', d_bf, w_mat, preferred_element_type=jnp.float32)  103 us
    dot_general x1, matrix products, attn_backward(): jnp.einsum('bhqk,bqhd->bkhd', d_score, q_r, preferred_element_type=jnp.fl...  86.9 us
    dot_general x1, matrix products, attn_backward(): jnp.einsum('bhqk,bkhd->bqhd', d_score, k_r, preferred_element_type=jnp.fl...  86.8 us
    dot_general x1, matrix products, layer_body(): jnp.einsum('bse,fe->bsf', dy_full, w_down, preferred_element_type=jnp.flo...  85.5 us
    all_gather x1, waiting for transfers between devices, layer_body(): dy_full = lax.all_gather(dy_blk, 'tp', axis=1, tiled=True)  83.8 us
    dot_general x3, matrix products, project(): jnp.einsum('bsd,de->bse', h_full, w_mat, preferred_element_type=jnp.float32)  77 us
  transfers between devices with their start and end apart: 4, of which 3 were waited for; matrix products, arithmetic and copies ran while one was open for 32% of the time, Pallas kernels for 0%

commit v1 on v0

v1 whole, which is shorter than its diff:
```python
import functools

import jax
import jax.numpy as jnp
from jax import lax
from jax.experimental import pallas as pl
from jax.experimental.pallas import tpu as pltpu
from jax.sharding import PartitionSpec as P

LN_EPS = 1e-5
CHUNK_PARTS = (1, 1, 1, 1)
LOG2E = 1.4426950408889634
GELU_A, GELU_B = 0.7978845608028654, 0.044715
F32, BF16 = jnp.float32, jnp.bfloat16


def dot_t(a, b, dims):
    return lax.dot_general(a, b, (dims, ((), ())), preferred_element_type=F32)


def call(kernel, name, grid, ins, outs, flops, full=()):
    arrays, specs = [a for a, _ in ins], [s for _, s in ins]
    first = len(outs) - len(full)
    aliases = {}
    for i, prev in enumerate(full):
        if prev is not None:
            aliases[len(arrays)] = first + i
            arrays.append(prev)
            specs.append(pl.BlockSpec(memory_space=pl.ANY))
    n_in = len(ins)

    def body(*refs):
        kernel(*refs[:n_in], *refs[len(arrays):])

    moved = sum(a.size * a.dtype.itemsize for a, _ in ins)
    return pl.pallas_call(
        body, grid=grid, in_specs=specs, out_specs=[s for _, _, s in outs],
        out_shape=[jax.ShapeDtypeStruct(s, d) for s, d, _ in outs], input_output_aliases=aliases,
        cost_estimate=pl.CostEstimate(flops=flops, bytes_accessed=moved, transcendentals=0), name=name)(*arrays)


def attn_kernel(heads, head_dim, half_rot, qkv_ref, dctx_ref, cos_ref, sin_ref, ctx_ref, dqkv_ref, bsum_ref, ctx_all_ref, dqkv_all_ref):
    seq_len = qkv_ref.shape[1]
    half = seq_len // 2
    width = heads * head_dim
    scale = head_dim ** -0.5
    cos_t, sin_t = cos_ref[...], sin_ref[...]
    mask = (lax.broadcasted_iota(jnp.int32, (half, half), 0) <= lax.broadcasted_iota(jnp.int32, (half, half), 1))

    def rope(t, sin_s):
        turned = jnp.concatenate([-t[:, half_rot:2 * half_rot], t[:, :half_rot], t[:, 2 * half_rot:]], axis=-1)
        return t * cos_t + turned * sin_s

    @pl.when(pl.program_id(0) == 0)
    def _():
        bsum_ref[...] = jnp.zeros_like(bsum_ref)

    for i in range(heads):
        cols = [slice(w * width + i * head_dim, w * width + (i + 1) * head_dim) for w in range(3)]
        own = cols[0]
        q = rope(qkv_ref[0, :, cols[0]].astype(F32), sin_t).astype(BF16)
        k = rope(qkv_ref[0, :, cols[1]].astype(F32), sin_t).astype(BF16)
        v = qkv_ref[0, :, cols[2]]
        d_ctx = dctx_ref[0, :, own]
        k_t, v_t = k.T, v.T
        ctx_t, dq_t, dk, dv = [], [], [], []
        for b in range(2):
            rows = slice(b * half, (b + 1) * half)
            keys = (b + 1) * half
            s = dot_t(k[:keys], q[rows], ((1,), (1,)))
            diag = jnp.where(mask, s[b * half:], -1e30)
            s = diag if b == 0 else jnp.concatenate([s[:half], diag], axis=0)
            e = jnp.exp2((s - jnp.max(s, axis=0, keepdims=True)) * (scale * LOG2E))
            prob = e * (1.0 / jnp.sum(e, axis=0, keepdims=True))
            prob_bf = prob.astype(BF16)
            ctx_t.append(dot_t(v_t[:, :keys], prob_bf, ((1,), (0,))).astype(BF16))
            d_prob = dot_t(v[:keys], d_ctx[rows], ((1,), (1,)))
            d_score = (prob * (d_prob - jnp.sum(d_prob * prob, axis=0, keepdims=True)) * scale).astype(BF16)
            dq_t.append(dot_t(k_t[:, :keys], d_score, ((1,), (0,))))
            dk.append(dot_t(d_score, q[rows], ((1,), (0,))))
            dv.append(dot_t(prob_bf, d_ctx[rows], ((1,), (0,))))
        ctx = jnp.concatenate(ctx_t, axis=1).T
        ctx_ref[0, :, own] = ctx
        ctx_all_ref[:, own] = ctx
        d_q = rope(jnp.concatenate(dq_t, axis=1).T, -sin_t)
        d_k = rope(jnp.concatenate([dk[0] + dk[1][:half], dk[1][half:]], axis=0), -sin_t)
        d_v = jnp.concatenate([dv[0] + dv[1][:half], dv[1][half:]], axis=0)
        for d_p, col in zip((d_q, d_k, d_v), cols):
            dqkv_ref[0, :, col] = d_p.astype(BF16)
            dqkv_all_ref[:, col] = d_p.astype(BF16)
            bsum_ref[:, col] += jnp.sum(d_p, axis=0, keepdims=True)


def attention(qkv, d_ctx, cos_full, sin_full, heads, head_dim, half_rot, seq0, total, full):
    n_seq, seq_len, width3 = qkv.shape
    width = heads * head_dim
    tab = pl.BlockSpec((seq_len, head_dim), lambda i: (0, 0))
    block = lambda w: pl.BlockSpec((1, seq_len, w), lambda i: (i, 0, 0))
    rows = lambda w: pl.BlockSpec((seq_len, w), lambda i: (i + seq0, 0))
    return call(functools.partial(attn_kernel, heads, head_dim, half_rot), "attention", (n_seq,),
                [(qkv, block(width3)), (d_ctx, block(width)), (cos_full, tab), (sin_full, tab)],
                [((n_seq, seq_len, width), BF16, block(width)), ((n_seq, seq_len, width3), BF16, block(width3)),
                 ((1, width3), F32, pl.BlockSpec((1, width3), lambda i: (0, 0))),
                 ((total, width), BF16, rows(width)), ((total, width3), BF16, rows(width3))],
                n_seq * heads * 4 * 2 * seq_len * seq_len * 256, full)


def const(arr):
    return (arr, pl.BlockSpec(arr.shape, lambda i: (0, 0)))


def normalize(x):
    x_f = x.astype(F32)
    centered = x_f - jnp.mean(x_f, axis=-1, keepdims=True)
    inv_std = lax.rsqrt(jnp.mean(centered * centered, axis=-1, keepdims=True) + LN_EPS)
    return centered * inv_std, inv_std


def ln_fwd_kernel(x_ref, gain_ref, bias_ref, h_ref):
    normed, _ = normalize(x_ref[0])
    h_ref[0] = (normed * gain_ref[...] + bias_ref[...]).astype(BF16)


def ln_bwd_kernel(x_ref, dy_ref, dh_ref, gain_ref, sums_ref, dx_ref):
    @pl.when(pl.program_id(0) == 0)
    def _():
        sums_ref[...] = jnp.zeros_like(sums_ref)

    normed, inv_std = normalize(x_ref[0])
    d_h, dy = dh_ref[0].astype(F32), dy_ref[0].astype(F32)
    d_norm = d_h * gain_ref[...]
    sums_ref[0:1] += jnp.sum(d_h * normed, axis=0, keepdims=True)
    sums_ref[1:2] += jnp.sum(d_h, axis=0, keepdims=True)
    sums_ref[2:3] += jnp.sum(dy, axis=0, keepdims=True)
    dx_ref[0] = dy + inv_std * (d_norm - jnp.mean(d_norm, axis=-1, keepdims=True)
                                - normed * jnp.mean(d_norm * normed, axis=-1, keepdims=True))


def residual_kernel(x_ref, part_ref, bo_ref, bdown_ref, y_ref):
    y_ref[0] = (x_ref[0].astype(F32) + part_ref[0].astype(F32) + bo_ref[...] + bdown_ref[...]).astype(BF16)


def front_h_kernel(tile, h_ref, wqkv_ref, bqkv_ref, wup_ref, bup_ref, qkv_ref, act_ref, slope_ref, act_all_ref, h_all_ref):
    h = h_ref[...]
    h_all_ref[...] = h
    for j in range(act_ref.shape[1] // tile):
        cols = slice(j * tile, (j + 1) * tile)
        t = jnp.dot(h, wup_ref[:, cols], preferred_element_type=F32) + bup_ref[:, cols]
        t2 = t * t
        th = jnp.tanh(t * (GELU_A + (GELU_A * GELU_B) * t2))
        half_t = 0.5 * t
        act = (half_t + half_t * th).astype(BF16)
        act_ref[:, cols] = act
        act_all_ref[:, cols] = act
        slope_ref[:, cols] = 0.5 + 0.5 * th + half_t * (1.0 - th * th) * (GELU_A + (3 * GELU_A * GELU_B) * t2)
    n = qkv_ref.shape[1]
    for j in range(0, n, tile):
        cols = slice(j, min(j + tile, n))
        qkv_ref[:, cols] = (jnp.dot(h, wqkv_ref[:, cols], preferred_element_type=F32) + bqkv_ref[:, cols]).astype(BF16)


def front_h(h, w_qkv, b_qkv, w_up, b_up, row0, total, full, bm=512, tile=256):
    rows, d = h.shape
    n1, n2 = w_qkv.shape[1], w_up.shape[1]
    blk = lambda c: pl.BlockSpec((bm, c), lambda i: (i, 0))
    off = lambda c: pl.BlockSpec((bm, c), lambda i: (i + row0 // bm, 0))
    return call(functools.partial(front_h_kernel, tile), "front_h", (rows // bm,),
                [(h, blk(d)), const(w_qkv), const(b_qkv), const(w_up), const(b_up)],
                [((rows, n1), BF16, blk(n1)), ((rows, n2), BF16, blk(n2)), ((rows, n2), F32, blk(n2)),
                 ((total, n2), BF16, off(n2)), ((total, d), BF16, off(d))], 2 * rows * d * (n1 + n2), full)


def front_d_kernel(tile, dy_ref, wo_ref, wdown_ref, slope_ref, dctx_ref, dpre_ref, bsum_ref, dpre_all_ref, dy_all_ref):
    @pl.when(pl.program_id(0) == 0)
    def _():
        bsum_ref[...] = jnp.zeros_like(bsum_ref)

    dy = dy_ref[...]
    dy_all_ref[...] = dy
    for j in range(dpre_ref.shape[1] // tile):
        cols = slice(j * tile, (j + 1) * tile)
        d_pre = dot_t(dy, wdown_ref[cols, :], ((1,), (1,))) * slope_ref[:, cols]
        bsum_ref[:, cols] += jnp.sum(d_pre, axis=0, keepdims=True)
        dpre_ref[:, cols] = d_pre.astype(BF16)
        dpre_all_ref[:, cols] = d_pre.astype(BF16)
    dctx_ref[...] = dot_t(dy, wo_ref[...], ((1,), (1,))).astype(BF16)


def front_d(dy, w_o, w_down, slope, row0, total, full, bm=512, tile=256):
    rows, d = dy.shape
    n1, n2 = w_o.shape[0], w_down.shape[0]
    blk = lambda c: pl.BlockSpec((bm, c), lambda i: (i, 0))
    off = lambda c: pl.BlockSpec((bm, c), lambda i: (i + row0 // bm, 0))
    return call(functools.partial(front_d_kernel, tile), "front_d", (rows // bm,),
                [(dy, blk(d)), const(w_o), const(w_down), (slope, blk(n2))],
                [((rows, n1), BF16, blk(n1)), ((rows, n2), BF16, blk(n2)),
                 ((1, n2), F32, pl.BlockSpec((1, n2), lambda i: (0, 0))),
                 ((total, n2), BF16, off(n2)), ((total, d), BF16, off(d))], 2 * rows * d * (n1 + n2), full)


def pair_kernel(tile, a_ref, b_ref, wa_ref, wb_ref, out_ref):
    for j in range(out_ref.shape[1] // tile):
        cols = slice(j * tile, (j + 1) * tile)
        out_ref[:, cols] = (jnp.dot(a_ref[...], wa_ref[:, cols], preferred_element_type=F32)
                            + jnp.dot(b_ref[...], wb_ref[:, cols], preferred_element_type=F32)).astype(BF16)


def pair_matmul(a, b, wa, wb, name, bm=512, tile=256):
    rows, ka = a.shape
    kb, n = wb.shape
    blk = lambda c: pl.BlockSpec((bm, c), lambda i: (i, 0))
    return call(functools.partial(pair_kernel, tile), name, (rows // bm,),
                [(a, blk(ka)), (b, blk(kb)), const(wa), const(wb)], [((rows, n), BF16, blk(n))],
                2 * rows * (ka + kb) * n)[0]


def layer_body(x_blk, rope_angle, ln_gain, ln_bias, w_q, b_q, w_k, b_k, w_v, b_v, w_o, b_o, w_up, b_up, w_down, b_down, dy_blk):
    n_seq, s_loc, model_dim = x_blk.shape
    seq_len, half_rot = rope_angle.shape
    heads, head_dim = b_q.shape
    width = heads * head_dim
    total = n_seq * seq_len

    pad = head_dim - 2 * half_rot
    cos_full = jnp.concatenate([jnp.cos(rope_angle)] * 2 + [jnp.ones((seq_len, pad), F32)], axis=-1)
    sin_full = jnp.concatenate([jnp.sin(rope_angle)] * 2 + [jnp.zeros((seq_len, pad), F32)], axis=-1)
    w_qkv = jnp.concatenate([w_q, w_k, w_v], axis=1)
    b_qkv = jnp.concatenate([b_q.reshape(1, -1), b_k.reshape(1, -1), b_v.reshape(1, -1)], axis=1)
    w_qkv_t, w_up_t = w_qkv.T, w_up.T

    edges = [0]
    for part in CHUNK_PARTS:
        edges.append(edges[-1] + n_seq * part // sum(CHUNK_PARTS))
    chunks = [slice(a, b) for a, b in zip(edges[:-1], edges[1:])]
    row3 = lambda off=0: pl.BlockSpec((1, s_loc, model_dim), lambda i: (i + off, 0, 0))
    gain, bias, bo, bdown = (t.reshape(1, -1) for t in (ln_gain, ln_bias, b_o, b_down))
    h_full, dy_full = [], []
    for sl in chunks:
        n = sl.stop - sl.start
        h_loc = call(ln_fwd_kernel, "ln_fwd", (n,), [(x_blk, row3(sl.start)), const(gain), const(bias)],
                     [((n, s_loc, model_dim), BF16, row3())], n * s_loc * model_dim * 200)[0]
        h_full.append(lax.all_gather(h_loc, 'tp', axis=1, tiled=True))
        dy_full.append(lax.all_gather(dy_blk[sl], 'tp', axis=1, tiled=True))

    bsum, bup_sum, small = 0, 0, 0
    y_all = dx_all = None
    act_all = h_all = dpre_all = dy_all = ctx_all = dqkv_all = None
    tie = None
    for c, sl in enumerate(chunks):
        per = sl.stop - sl.start
        rows, row0 = per * seq_len, sl.start * seq_len
        h, dy = h_full[c].reshape(rows, model_dim), dy_full[c].reshape(rows, model_dim)
        if tie is not None:
            h, tie = lax.optimization_barrier((h, tie))
        qkv, act, slope, act_all, h_all = front_h(h, w_qkv, b_qkv, w_up, b_up.reshape(1, -1), row0, total, (act_all, h_all))
        d_ctx, d_pre, b_part, dpre_all, dy_all = front_d(dy, w_o, w_down, slope, row0, total, (dpre_all, dy_all))
        bup_sum += b_part[0]
        ctx, d_qkv, b_part, ctx_all, dqkv_all = attention(
            qkv.reshape(per, seq_len, 3 * width), d_ctx.reshape(per, seq_len, width), cos_full, sin_full,
            heads, head_dim, half_rot, sl.start, total, (ctx_all, dqkv_all))
        bsum += b_part[0]
        ctx, d_qkv = ctx.reshape(rows, width), d_qkv.reshape(rows, 3 * width)
        branch = pair_matmul(ctx, act, w_o, w_down, "branch")
        d_qkv, branch = lax.optimization_barrier((d_qkv, branch))
        d_h = pair_matmul(d_qkv, d_pre, w_qkv_t, w_up_t, "d_h")
        tie = d_h
        branch_sum = lax.psum_scatter(branch.reshape(per, seq_len, model_dim), 'tp', scatter_dimension=1, tiled=True)
        y_all = call(residual_kernel, "residual", (per,), [(x_blk, row3(sl.start)), (branch_sum, row3()), const(bo), const(bdown)],
                     [((n_seq, s_loc, model_dim), BF16, row3(sl.start))], per * s_loc * model_dim * 100, (y_all,))[0]
        d_h_loc = lax.psum_scatter(d_h.reshape(per, seq_len, model_dim), 'tp', scatter_dimension=1, tiled=True)
        d_h_loc, y_all = lax.optimization_barrier((d_h_loc, y_all))
        part, dx_all = call(ln_bwd_kernel, "ln_bwd", (per,),
                            [(x_blk, row3(sl.start)), (dy_blk, row3(sl.start)), (d_h_loc, row3()), const(gain)],
                            [((8, model_dim), F32, pl.BlockSpec((8, model_dim), lambda i: (0, 0))),
                             ((n_seq, s_loc, model_dim), F32, row3(sl.start))], per * s_loc * model_dim * 200, (dx_all,))
        small += part[:3]
    h_all, dy_all, act_all, ctx_all, tie = lax.optimization_barrier((h_all, dy_all, act_all, ctx_all, tie))
    t0 = ((0,), (0,))
    g_o = dot_t(ctx_all, dy_all, t0)
    g_down = dot_t(act_all, dy_all, t0)
    g_qkv = dot_t(h_all, dqkv_all, t0)
    g_up = dot_t(h_all, dpre_all, t0)
    small = lax.psum(small, 'tp')
    bsum = bsum.reshape(3, heads, head_dim)
    return (y_all, dx_all, small[0], small[1],
            g_qkv[:, :width], bsum[0], g_qkv[:, width:2 * width], bsum[1], g_qkv[:, 2 * width:], bsum[2],
            g_o, small[2], g_up, bup_sum, g_down, small[2])


def solution(mesh):
    row_spec = P('dp', 'tp', None)
    col_spec = P(None, 'tp')
    head_spec = P('tp', None)
    grad_cols = P('dp', 'tp')
    grad_rows = P(('dp', 'tp'), None)
    in_specs = (row_spec, P(None, None), P(None), P(None), col_spec, head_spec, col_spec, head_spec,
                col_spec, head_spec, P('tp', None), P(None), col_spec, P('tp'), P('tp', None), P(None), row_spec)
    out_specs = (row_spec, row_spec, P('dp'), P('dp'), grad_cols, grad_rows, grad_cols, grad_rows, grad_cols,
                 grad_rows, grad_rows, P('dp'), grad_cols, P(('dp', 'tp')), grad_rows, P('dp'))
    return jax.shard_map(layer_body, mesh=mesh, in_specs=in_specs, out_specs=out_specs, check_vma=False)
```

time: 1540 us -> 1020 us (0.66)
  matrix products: 1090 us -> 202 us
  Pallas kernels: 0 us -> 678 us
  waiting for transfers between devices: 298 us -> 42.4 us
  other arithmetic: 87.6 us -> 3.21 us
  local copies, waits for them, and re-layouts: 19.8 us -> 47.5 us
    dot_general x23 -> x4, matrix products: 1060 us -> 202 us  [dot_t(): return lax.dot_general(a, b, (dims, ((), ())), preferred_element_type=F32)]
    pallas_call x0 -> x32, Pallas kernels: none -> 678 us  [call(): pl.pallas_call(body, grid=grid, in_specs=specs, out_specs=[s for _, _, s...]
    all_gather x2 -> x8, waiting for transfers between devices: 273 us -> 39.8 us  [the longest x4 20.8 us: layer_body(): dy_full.append(lax.all_gather(dy_blk[sl], 'tp', axis=1, tiled=True))]
    reduce_sum x7 -> x0, other arithmetic: 43.3 us -> none  [the longest x1 16.9 us: layer_body(): jnp.sum(dy_f, axis=(0, 1))]
    sub x1 -> x0, matrix products: 36.6 us -> none  [attn_forward(): prob_f = jax.nn.softmax(jnp.where(causal, scores, -1e+30), axis=-1)]
    convert_element_type x6 -> x0, other arithmetic: 28.9 us -> none  [the longest x2 14.8 us: layer_body(): d_proj.astype(jnp.bfloat16).reshape(n_seq, seq_len, heads_loc * head_dim)]
    reduce_scatter x2 -> x8, waiting for transfers between devices: 24.4 us -> 0.01 us  [the longest x4 0.01 us: layer_body(): lax.psum_scatter(branch.reshape(per, seq_len, model_dim), 'tp', scatter_d...]
  transfers between devices with their start and end apart: 4 -> 16, of which waited for: 3 -> 2; matrix products, arithmetic and copies ran while one was open for 32% -> 24% of each run, Pallas kernels for 0% -> 64%
where the time goes in v1:
time: 1020 us; the launch traced here: 1010 us
  Pallas kernels  678 us (66%)
  matrix products  202 us (20%)
  local copies, waits for them, and re-layouts  47.5 us (5%)
  waiting for transfers between devices  42.4 us (4%)
  blocking collectives  24.7 us (2%)
  between operations  14.4 us (1%)
    pallas_call x32, Pallas kernels, call(): pl.pallas_call(body, grid=grid, in_specs=specs, out_specs=[s for _, _, s...  678 us
    dot_general x4, matrix products, dot_t(): return lax.dot_general(a, b, (dims, ((), ())), preferred_element_type=F32)  202 us
    psum x1, blocking collectives, layer_body(): small = lax.psum(small, 'tp')  24.7 us
    all_gather x4, waiting for transfers between devices, layer_body(): dy_full.append(lax.all_gather(dy_blk[sl], 'tp', axis=1, tiled=True))  20.8 us
  transfers between devices with their start and end apart: 16, of which 2 were waited for; matrix products, arithmetic and copies ran while one was open for 24% of the time, Pallas kernels for 64%

profile of v1, /device:TPU:112, one launch (start us, length us, event | category | flops | bytes accessed | tf_op | source)
XLA Modules:
  0.0 1013.6 jit_solution(13023056492764301870)
XLA Ops:
  7.3 1.3 reshape.186.refs_1_.refs_3_
  8.6 1.3 reshape.187.refs_2_
  9.9 4.1 ln_fwd.7
  14.1 4.9 fusion.1
  19.2 4.1 ln_fwd.6
  24.0 4.1 ln_fwd.5
  28.9 4.2 ln_fwd.4
  33.2 0.7 all-gather.23.cloned.1.call-update
  35.9 0.8 fusion.2
  36.6 0.9 copy.67
  37.5 1.6 copy.65
  39.1 1.3 constant_dynamic-update-slice_fusion.2
  40.4 1.3 constant_dynamic-update-slice_fusion.1
  41.7 1.3 constant_dynamic-update-slice_fusion
  42.9 7.8 copy.64.refs_1_
  50.8 0.7 pad_maximum_fusion.refs_2_
  51.5 1.0 maximum_maximum_fusion
  52.5 18.9 %all-gather.15.cloned.1.call-done = bf16[4,512,2560]{2,1,0:T(8,128)(2,1)} async-done(((bf16[4,64,2560]{2,1,0:T(8,128)(2,1)}), bf16[4,512,2560]{2,1,0:T(8,128)(2,1)}) %all-gather.15.cloned.1.call-update) | async-done | bytes 10485776 | tf_op jit(solution)/shard_map/all_gather | solution.py:242
  71.4 36.0 %front_h.4 = (bf16[2048,960]{1,0:T(8,128)(2,1)}, bf16[2048,1280]{1,0:T(8,128)(2,1)}, f32[2048,1280]{1,0:T(8,128)}, bf16[8192,1280]{1,0:T(8,128)(2,1)}, bf16[8192,2560]{1,0:T(8,128)(2,1)}) custom-call(bf16[2048,2560]{1,0:T(8,128)(2,1)} %bitcast.60, bf16[2560,960]{1,0:T(8,128)(2,1)} %copy.64.refs_1_, f32[1,960]{1,0:T(1,128)} %pad_maximum_fusion.refs_2_, ...), custom_call_target="tpu_custom_call" | custom-call | flops 23488102400 | bytes 21963520 | tf_op jit(solution)/shard_map/front_h/pallas_call | solution.py:36
  107.4 20.8 %all-gather.17.cloned.1.call-done = bf16[4,512,2560]{2,1,0:T(8,128)(2,1)} async-done(((bf16[4,64,2560]{2,1,0:T(8,128)(2,1)}), bf16[4,512,2560]{2,1,0:T(8,128)(2,1)}) %all-gather.17.cloned.1.call-update) | async-done | bytes 10485776 | tf_op jit(solution)/shard_map/all_gather | solution.py:243
  128.2 25.9 %front_d.4 = (bf16[2048,320]{1,0:T(8,128)(2,1)}, bf16[2048,1280]{1,0:T(8,128)(2,1)}, f32[1,1280]{1,0:T(1,128)}, bf16[8192,1280]{1,0:T(8,128)(2,1)}, bf16[8192,2560]{1,0:T(8,128)(2,1)}) custom-call(bf16[2048,2560]{1,0:T(8,128)(2,1)} %bitcast.61, bf16[320,2560]{1,0:T(8,128)(2,1)} %refs_2_.15, bf16[1280,2560]{1,0:T(8,128)(2,1)} %refs_3_.15, ...), custom_call_target="tpu_custom_call" | custom-call | flops 16777216000 | bytes 29163520 | tf_op jit(solution)/shard_map/front_d/pallas_call | solution.py:36
  154.1 36.9 %attention.4 = (bf16[4,512,320]{2,1,0:T(8,128)(2,1)}, bf16[4,512,960]{2,1,0:T(8,128)(2,1)}, f32[1,960]{1,0:T(1,128)}, bf16[8192,320]{1,0:T(8,128)(2,1)}, bf16[8192,960]{1,0:T(8,128)(2,1)}) custom-call(bf16[4,512,960]{2,1,0:T(8,128)(2,1)} %bitcast.69, bf16[4,512,320]{2,1,0:T(8,128)(2,1)} %bitcast.73, f32[512,80]{1,0:T(8,128)} %get-tuple-element.213.refs_2_, ...), custom_call_target="tpu_custom_call" | custom-call | flops 8589934592 | bytes 5570560 | tf_op jit(solution)/shard_map/attention/pallas_call | solution.py:36
  191.0 25.0 %branch.4 = bf16[2048,2560]{1,0:T(8,128)(2,1)} custom-call(bf16[2048,320]{1,0:T(8,128)(2,1)} %bitcast.77, bf16[2048,1280]{1,0:T(8,128)(2,1)} %get-tuple-element.112.refs_1_, bf16[320,2560]{1,0:T(8,128)(2,1)} %refs_2_.15, bf16[1280,2560]{1,0:T(8,128)(2,1)} %refs_3_.15), custom_call_target="tpu_custom_call" | custom-call | flops 16777216000 | bytes 14745600 | tf_op jit(solution)/shard_map/branch/pallas_call | solution.py:36
  216.1 9.7 copy.69
  225.8 31.6 %d_h.4 = bf16[2048,2560]{1,0:T(8,128)(2,1)} custom-call(bf16[2048,960]{1,0:T(8,128)(2,1)} %bitcast.72, bf16[2048,1280]{1,0:T(8,128)(2,1)} %get-tuple-element.114.refs_1_, bf16[960,2560]{1,0:T(8,128)(2,1)} %bitcast.9.refs_2_, bf16[1280,2560]{1,0:T(8,128)(2,1)} %bitcast.53), custom_call_target="tpu_custom_call" | custom-call | flops 23488102400 | bytes 20643840 | tf_op jit(solution)/shard_map/d_h/pallas_call | solution.py:36
  257.6 36.1 %front_h.5 = (bf16[2048,960]{1,0:T(8,128)(2,1)}, bf16[2048,1280]{1,0:T(8,128)(2,1)}, f32[2048,1280]{1,0:T(8,128)}, bf16[8192,1280]{1,0:T(8,128)(2,1)}, bf16[8192,2560]{1,0:T(8,128)(2,1)}) custom-call(bf16[2048,2560]{1,0:T(8,128)(2,1)} %bitcast.59, bf16[2560,960]{1,0:T(8,128)(2,1)} %copy.64.refs_1_, ...), custom_call_target="tpu_custom_call", output_to_operand_aliasing={{3}: (5, {}), {4}: (6, {})} | custom-call | flops 23488102400 | bytes 21963520 | tf_op jit(solution)/shard_map/front_h/pallas_call | solution.py:36
  293.7 26.0 %front_d.5 = (bf16[2048,320]{1,0:T(8,128)(2,1)}, bf16[2048,1280]{1,0:T(8,128)(2,1)}, f32[1,1280]{1,0:T(1,128)}, bf16[8192,1280]{1,0:T(8,128)(2,1)}, bf16[8192,2560]{1,0:T(8,128)(2,1)}) custom-call(bf16[2048,2560]{1,0:T(8,128)(2,1)} %bitcast.44, bf16[320,2560]{1,0:T(8,128)(2,1)} %refs_2_.15, ...), custom_call_target="tpu_custom_call", output_to_operand_aliasing={{3}: (4, {}), {4}: (5, {})} | custom-call | flops 16777216000 | bytes 29163520 | tf_op jit(solution)/shard_map/front_d/pallas_call | solution.py:36
  319.7 36.6 %attention.5 = (bf16[4,512,320]{2,1,0:T(8,128)(2,1)}, bf16[4,512,960]{2,1,0:T(8,128)(2,1)}, f32[1,960]{1,0:T(1,128)}, bf16[8192,320]{1,0:T(8,128)(2,1)}, bf16[8192,960]{1,0:T(8,128)(2,1)}) custom-call(bf16[4,512,960]{2,1,0:T(8,128)(2,1)} %bitcast.67, bf16[4,512,320]{2,1,0:T(8,128)(2,1)} %bitcast.63, ...), custom_call_target="tpu_custom_call", output_to_operand_aliasing={{3}: (4, {}), {4}: (5, {})} | custom-call | flops 8589934592 | bytes 5570560 | tf_op jit(solution)/shard_map/attention/pallas_call | solution.py:36
  356.3 25.0 %branch.5 = bf16[2048,2560]{1,0:T(8,128)(2,1)} custom-call(bf16[2048,320]{1,0:T(8,128)(2,1)} %bitcast.75, bf16[2048,1280]{1,0:T(8,128)(2,1)} %get-tuple-element.127.refs_1_, bf16[320,2560]{1,0:T(8,128)(2,1)} %refs_2_.15, bf16[1280,2560]{1,0:T(8,128)(2,1)} %refs_3_.15), custom_call_target="tpu_custom_call" | custom-call | flops 16777216000 | bytes 14745600 | tf_op jit(solution)/shard_map/branch/pallas_call | solution.py:36
  381.4 32.0 %d_h.5 = bf16[2048,2560]{1,0:T(8,128)(2,1)} custom-call(bf16[2048,960]{1,0:T(8,128)(2,1)} %bitcast.70, bf16[2048,1280]{1,0:T(8,128)(2,1)} %get-tuple-element.129.refs_1_, bf16[960,2560]{1,0:T(8,128)(2,1)} %bitcast.9.refs_2_, bf16[1280,2560]{1,0:T(8,128)(2,1)} %bitcast.54), custom_call_target="tpu_custom_call" | custom-call | flops 23488102400 | bytes 20643840 | tf_op jit(solution)/shard_map/d_h/pallas_call | solution.py:36
  413.6 36.1 %front_h.6 = (bf16[2048,960]{1,0:T(8,128)(2,1)}, bf16[2048,1280]{1,0:T(8,128)(2,1)}, f32[2048,1280]{1,0:T(8,128)}, bf16[8192,1280]{1,0:T(8,128)(2,1)}, bf16[8192,2560]{1,0:T(8,128)(2,1)}) custom-call(bf16[2048,2560]{1,0:T(8,128)(2,1)} %bitcast.58, bf16[2560,960]{1,0:T(8,128)(2,1)} %copy.64.refs_1_, ...), custom_call_target="tpu_custom_call", output_to_operand_aliasing={{3}: (5, {}), {4}: (6, {})} | custom-call | flops 23488102400 | bytes 21963520 | tf_op jit(solution)/shard_map/front_h/pallas_call | solution.py:36
  449.7 26.0 %front_d.6 = (bf16[2048,320]{1,0:T(8,128)(2,1)}, bf16[2048,1280]{1,0:T(8,128)(2,1)}, f32[1,1280]{1,0:T(1,128)}, bf16[8192,1280]{1,0:T(8,128)(2,1)}, bf16[8192,2560]{1,0:T(8,128)(2,1)}) custom-call(bf16[2048,2560]{1,0:T(8,128)(2,1)} %bitcast.43, bf16[320,2560]{1,0:T(8,128)(2,1)} %refs_2_.15, ...), custom_call_target="tpu_custom_call", output_to_operand_aliasing={{3}: (4, {}), {4}: (5, {})} | custom-call | flops 16777216000 | bytes 29163520 | tf_op jit(solution)/shard_map/front_d/pallas_call | solution.py:36
  475.7 36.6 %attention.6 = (bf16[4,512,320]{2,1,0:T(8,128)(2,1)}, bf16[4,512,960]{2,1,0:T(8,128)(2,1)}, f32[1,960]{1,0:T(1,128)}, bf16[8192,320]{1,0:T(8,128)(2,1)}, bf16[8192,960]{1,0:T(8,128)(2,1)}) custom-call(bf16[4,512,960]{2,1,0:T(8,128)(2,1)} %bitcast.68, bf16[4,512,320]{2,1,0:T(8,128)(2,1)} %bitcast.64, ...), custom_call_target="tpu_custom_call", output_to_operand_aliasing={{3}: (4, {}), {4}: (5, {})} | custom-call | flops 8589934592 | bytes 5570560 | tf_op jit(solution)/shard_map/attention/pallas_call | solution.py:36
  512.2 25.1 %branch.6 = bf16[2048,2560]{1,0:T(8,128)(2,1)} custom-call(bf16[2048,320]{1,0:T(8,128)(2,1)} %bitcast.76, bf16[2048,1280]{1,0:T(8,128)(2,1)} %get-tuple-element.142.refs_1_, bf16[320,2560]{1,0:T(8,128)(2,1)} %refs_2_.15, bf16[1280,2560]{1,0:T(8,128)(2,1)} %refs_3_.15), custom_call_target="tpu_custom_call" | custom-call | flops 16777216000 | bytes 14745600 | tf_op jit(solution)/shard_map/branch/pallas_call | solution.py:36
  537.4 31.8 %d_h.6 = bf16[2048,2560]{1,0:T(8,128)(2,1)} custom-call(bf16[2048,960]{1,0:T(8,128)(2,1)} %bitcast.71, bf16[2048,1280]{1,0:T(8,128)(2,1)} %get-tuple-element.144.refs_1_, bf16[960,2560]{1,0:T(8,128)(2,1)} %bitcast.9.refs_2_, bf16[1280,2560]{1,0:T(8,128)(2,1)} %bitcast.55), custom_call_target="tpu_custom_call" | custom-call | flops 23488102400 | bytes 20643840 | tf_op jit(solution)/shard_map/d_h/pallas_call | solution.py:36
  569.4 36.1 %front_h.7 = (bf16[2048,960]{1,0:T(8,128)(2,1)}, bf16[2048,1280]{1,0:T(8,128)(2,1)}, f32[2048,1280]{1,0:T(8,128)}, bf16[8192,1280]{1,0:T(8,128)(2,1)}, bf16[8192,2560]{1,0:T(8,128)(2,1)}) custom-call(bf16[2048,2560]{1,0:T(8,128)(2,1)} %bitcast.57, bf16[2560,960]{1,0:T(8,128)(2,1)} %copy.64.refs_1_, ...), custom_call_target="tpu_custom_call", output_to_operand_aliasing={{3}: (5, {}), {4}: (6, {})} | custom-call | flops 23488102400 | bytes 21963520 | tf_op jit(solution)/shard_map/front_h/pallas_call | solution.py:36
  605.6 26.0 %front_d.7 = (bf16[2048,320]{1,0:T(8,128)(2,1)}, bf16[2048,1280]{1,0:T(8,128)(2,1)}, f32[1,1280]{1,0:T(1,128)}, bf16[8192,1280]{1,0:T(8,128)(2,1)}, bf16[8192,2560]{1,0:T(8,128)(2,1)}) custom-call(bf16[2048,2560]{1,0:T(8,128)(2,1)} %bitcast.42, bf16[320,2560]{1,0:T(8,128)(2,1)} %refs_2_.15, ...), custom_call_target="tpu_custom_call", output_to_operand_aliasing={{3}: (4, {}), {4}: (5, {})} | custom-call | flops 16777216000 | bytes 29163520 | tf_op jit(solution)/shard_map/front_d/pallas_call | solution.py:36
  631.5 36.9 %attention.7 = (bf16[4,512,320]{2,1,0:T(8,128)(2,1)}, bf16[4,512,960]{2,1,0:T(8,128)(2,1)}, f32[1,960]{1,0:T(1,128)}, bf16[8192,320]{1,0:T(8,128)(2,1)}, bf16[8192,960]{1,0:T(8,128)(2,1)}) custom-call(bf16[4,512,960]{2,1,0:T(8,128)(2,1)} %bitcast.66, bf16[4,512,320]{2,1,0:T(8,128)(2,1)} %bitcast.62, ...), custom_call_target="tpu_custom_call", output_to_operand_aliasing={{3}: (4, {}), {4}: (5, {})} | custom-call | flops 8589934592 | bytes 5570560 | tf_op jit(solution)/shard_map/attention/pallas_call | solution.py:36
  668.5 25.0 %branch.7 = bf16[2048,2560]{1,0:T(8,128)(2,1)} custom-call(bf16[2048,320]{1,0:T(8,128)(2,1)} %bitcast.74, bf16[2048,1280]{1,0:T(8,128)(2,1)} %get-tuple-element.157.refs_1_, bf16[320,2560]{1,0:T(8,128)(2,1)} %refs_2_.15, bf16[1280,2560]{1,0:T(8,128)(2,1)} %refs_3_.15), custom_call_target="tpu_custom_call" | custom-call | flops 16777216000 | bytes 14745600 | tf_op jit(solution)/shard_map/branch/pallas_call | solution.py:36
  694.2 0.6 reshape.218.refs_2_
  694.8 0.6 reshape.219.refs_3_
  695.5 0.7 slice.85
  696.2 0.7 slice.82
  696.8 0.7 slice.79
  697.5 31.5 %d_h.7 = bf16[2048,2560]{1,0:T(8,128)(2,1)} custom-call(bf16[2048,960]{1,0:T(8,128)(2,1)} %bitcast.65, bf16[2048,1280]{1,0:T(8,128)(2,1)} %get-tuple-element.159.refs_1_, bf16[960,2560]{1,0:T(8,128)(2,1)} %bitcast.9.refs_2_, bf16[1280,2560]{1,0:T(8,128)(2,1)} %bitcast.56), custom_call_target="tpu_custom_call" | custom-call | flops 23488102400 | bytes 20643840 | tf_op jit(solution)/shard_map/d_h/pallas_call | solution.py:36
  729.1 0.6 copy-done.12
  729.7 0.6 add_reduce_fusion
  730.4 50.9 %fusion.3 = f32[2560,960]{0,1:T(8,128)} fusion(bf16[8192,2560]{1,0:T(8,128)(2,1)} %get-tuple-element.184, bf16[8192,960]{1,0:T(8,128)(2,1)} %get-tuple-element.185), kind=kOutput, calls=%fused_computation.18 | convolution fusion | flops 40265318400 | bytes 67502080 | tf_op jit(solution)/shard_map/dot_general | solution.py:18
  781.3 7.9 fusion
  789.2 24.3 %fusion.4 = f32[320,2560]{1,0:T(8,128)} fusion(bf16[8192,320]{1,0:T(8,128)(2,1)} %get-tuple-element.190, bf16[8192,2560]{1,0:T(8,128)(2,1)} %get-tuple-element.191), kind=kOutput, calls=%fused_computation.19 | convolution fusion | flops 13421772800 | bytes 50462720 | tf_op jit(solution)/shard_map/dot_general | solution.py:18
  813.5 63.3 %fusion.5 = f32[2560,1280]{1,0:T(8,128)} fusion(bf16[8192,2560]{1,0:T(8,128)(2,1)} %get-tuple-element.184, bf16[8192,1280]{1,0:T(8,128)(2,1)} %get-tuple-element.192), kind=kOutput, calls=%fused_computation.20 | convolution fusion | flops 53687091200 | bytes 76021760 | tf_op jit(solution)/shard_map/dot_general | solution.py:18
  876.9 63.6 %fusion.6 = f32[1280,2560]{1,0:T(8,128)} fusion(bf16[8192,1280]{1,0:T(8,128)(2,1)} %get-tuple-element.197, bf16[8192,2560]{1,0:T(8,128)(2,1)} %get-tuple-element.191), kind=kOutput, calls=%fused_computation.21 | convolution fusion | flops 53687091200 | bytes 76021760 | tf_op jit(solution)/shard_map/dot_general | solution.py:18
  940.4 3.9 residual.4.refs_4_
  944.3 3.9 residual.5.refs_4_
  948.2 3.9 residual.6.refs_4_
  952.1 3.9 residual.7
  956.0 6.0 ln_bwd.4
  962.0 6.0 ln_bwd.5
  968.0 6.0 ln_bwd.6
  974.0 6.0 ln_bwd.7
  980.0 0.9 slice_add_fusion
  980.9 24.7 %psum.7 = f32[3,2560]{1,0:T(4,128)S(1)} all-reduce(f32[3,2560]{1,0:T(4,128)S(1)} %slice_add_fusion), channel_id=1, replica_groups=mesh['dp'=2,'tp'=8] {'tp'}, use_global_device_ids=true, to_apply=%region_8.0 | all-reduce | flops 7680 | bytes 61440 | tf_op jit(solution)/shard_map/psum | solution.py:283
  1005.6 0.7 slice_reduce_fusion
  1006.2 0.6 copy.100
  (102 shorter events, 5.6 us)
Async XLA Ops:
  7.2 64.2 %all-gather.15.cloned.1.call-start = ((), (), s32[]{:S(2)}) async-start(), calls=%async_computation.11 | async-start | bytes 11796480 | tf_op jit(solution)/shard_map/all_gather | solution.py:242
  14.0 114.2 %all-gather.17.cloned.1.call-start = ((), (), s32[]{:S(2)}) async-start(), calls=%async_computation.12 | async-start | bytes 11796480 | tf_op jit(solution)/shard_map/all_gather | solution.py:243
  19.1 238.5 %all-gather.13.cloned.1.call-start = ((), (), s32[]{:S(2)}) async-start(), calls=%async_computation.10 | async-start | bytes 11796480 | tf_op jit(solution)/shard_map/all_gather | solution.py:242
  23.3 270.4 %all-gather.19.cloned.1.call-start = ((), (), s32[]{:S(2)}) async-start(), calls=%async_computation.13 | async-start | bytes 11796480 | tf_op jit(solution)/shard_map/all_gather | solution.py:243
  23.9 389.7 %all-gather.11.cloned.1.call-start = ((), (), s32[]{:S(2)}) async-start(), calls=%async_computation.9 | async-start | bytes 11796480 | tf_op jit(solution)/shard_map/all_gather | solution.py:242
  28.1 6.9 copy-start.20
  28.1 7.0 copy-start.21
  28.1 7.1 copy-start.22
  28.1 7.2 copy-start.11
  28.1 7.8 copy-start.5
  28.1 11.0 %copy-start = (bf16[2560,320]{0,1:T(8,128)(2,1)S(1)}, bf16[2560,320]{0,1:T(8,128)(2,1)}, u32[]{:S(2)}) copy-start(bf16[2560,320]{0,1:T(8,128)(2,1)} %param.21) | copy-start | bytes 4915204
  28.2 421.5 %all-gather.21.cloned.1.call-start = ((), (), s32[]{:S(2)}) async-start(), calls=%async_computation.14 | async-start | bytes 11796480 | tf_op jit(solution)/shard_map/all_gather | solution.py:243
  28.8 11.6 %copy-start.1 = (bf16[2560,320]{0,1:T(8,128)(2,1)S(1)}, bf16[2560,320]{0,1:T(8,128)(2,1)}, u32[]{:S(2)}) copy-start(bf16[2560,320]{0,1:T(8,128)(2,1)} %param.23) | copy-start | bytes 4915204
  28.8 540.6 %all-gather.9.cloned.1.call-start = ((), (), s32[]{:S(2)}) async-start(), calls=%async_computation.8 | async-start | bytes 11796480 | tf_op jit(solution)/shard_map/all_gather | solution.py:242
  33.2 572.4 %all-gather.23.cloned.1.call-start = ((), (), s32[]{:S(2)}) async-start(), calls=%async_computation.15 | async-start | bytes 11796480 | tf_op jit(solution)/shard_map/all_gather | solution.py:243
  34.0 906.5 %reduce-scatter.23.cloned.1.call-start = ((), (), s32[]{:S(2)}) async-start(), calls=%async_computation.23 | async-start | bytes 11796480 | tf_op jit(solution)/shard_map/reduce_scatter | solution.py:267
  39.1 2.6 copy-start.2
  41.7 9.8 copy-start.3
  41.7 9.8 copy-start.23
  216.1 728.3 %reduce-scatter.21.cloned.1.call-start = ((), (), s32[]{:S(2)}) async-start(), calls=%async_computation.22 | async-start | bytes 11796480 | tf_op jit(solution)/shard_map/reduce_scatter | solution.py:270
  257.5 686.9 %reduce-scatter.19.cloned.1.call-start = ((), (), s32[]{:S(2)}) async-start(), calls=%async_computation.21 | async-start | bytes 11796480 | tf_op jit(solution)/shard_map/reduce_scatter | solution.py:267
  381.4 566.9 %reduce-scatter.17.cloned.1.call-start = ((), (), s32[]{:S(2)}) async-start(), calls=%async_computation.20 | async-start | bytes 11796480 | tf_op jit(solution)/shard_map/reduce_scatter | solution.py:270
  413.5 534.7 %reduce-scatter.15.cloned.1.call-start = ((), (), s32[]{:S(2)}) async-start(), calls=%async_computation.19 | async-start | bytes 11796480 | tf_op jit(solution)/shard_map/reduce_scatter | solution.py:267
  537.4 414.8 %reduce-scatter.13.cloned.1.call-start = ((), (), s32[]{:S(2)}) async-start(), calls=%async_computation.18 | async-start | bytes 11796480 | tf_op jit(solution)/shard_map/reduce_scatter | solution.py:270
  569.3 382.8 %reduce-scatter.11.cloned.1.call-start = ((), (), s32[]{:S(2)}) async-start(), calls=%async_computation.17 | async-start | bytes 11796480 | tf_op jit(solution)/shard_map/reduce_scatter | solution.py:267
  693.5 0.7 copy-start.9
  693.5 1.3 copy-start.10
  693.5 1.9 copy-start.16
  693.5 1.9 copy-start.17
  693.5 1.9 copy-start.18
  693.5 1.9 copy-start.19
  693.6 262.5 %reduce-scatter.9.cloned.1.call-start = ((), (), s32[]{:S(2)}) async-start(), calls=%async_computation.16 | async-start | bytes 11796480 | tf_op jit(solution)/shard_map/reduce_scatter | solution.py:270
  729.0 0.7 copy-start.12
  729.0 0.7 copy-start.13
  729.0 0.7 copy-start.14
  729.0 0.7 copy-start.15
  973.9 6.0 copy-start.6
  973.9 6.0 copy-start.7
  973.9 6.0 copy-start.8
  1006.2 0.6 copy-start.4
Sparse Core Ops, SparseCore 0:
  14.1 57.1 all-gather.14
  73.5 54.6 all-gather.16
  129.8 54.6 all-gather.12
  185.9 54.6 all-gather.18
  242.6 54.6 all-gather.10
  298.7 54.6 all-gather.20
  355.5 54.6 all-gather.8
  411.8 54.6 all-gather.22
  468.7 58.6 reduce-scatter.22
  529.6 58.0 reduce-scatter.20
  590.0 58.0 reduce-scatter.18
  650.3 58.0 reduce-scatter.16
  710.7 58.0 reduce-scatter.14
  770.9 58.0 reduce-scatter.12
  831.8 58.0 reduce-scatter.10
  892.0 58.0 reduce-scatter.8

commit v2 on v1

--- a/solution.py
+++ b/solution.py
@@ -8,7 +8,7 @@
 from jax.sharding import PartitionSpec as P
 
 LN_EPS = 1e-5
-CHUNK_PARTS = (1, 1, 1, 1)
+CHUNK_PARTS = (3, 5, 8)
 LOG2E = 1.4426950408889634
 GELU_A, GELU_B = 0.7978845608028654, 0.044715
 F32, BF16 = jnp.float32, jnp.bfloat16
@@ -55,40 +55,62 @@
     def _():
         bsum_ref[...] = jnp.zeros_like(bsum_ref)
 
-    for i in range(heads):
-        cols = [slice(w * width + i * head_dim, w * width + (i + 1) * head_dim) for w in range(3)]
-        own = cols[0]
+    units = [(i, b) for i in range(heads) for b in range(2)]
+    loaded, scored, soft, acc = {}, {}, {}, {}
+
+    def head_cols(i):
+        return [slice(w * width + i * head_dim, w * width + (i + 1) * head_dim) for w in range(3)]
+
+    def load_head(i):
+        cols = head_cols(i)
         q = rope(qkv_ref[0, :, cols[0]].astype(F32), sin_t).astype(BF16)
         k = rope(qkv_ref[0, :, cols[1]].astype(F32), sin_t).astype(BF16)
         v = qkv_ref[0, :, cols[2]]
-        d_ctx = dctx_ref[0, :, own]
-        k_t, v_t = k.T, v.T
-        ctx_t, dq_t, dk, dv = [], [], [], []
-        for b in range(2):
-            rows = slice(b * half, (b + 1) * half)
-            keys = (b + 1) * half
-            s = dot_t(k[:keys], q[rows], ((1,), (1,)))
-            diag = jnp.where(mask, s[b * half:], -1e30)
-            s = diag if b == 0 else jnp.concatenate([s[:half], diag], axis=0)
-            e = jnp.exp2((s - jnp.max(s, axis=0, keepdims=True)) * (scale * LOG2E))
-            prob = e * (1.0 / jnp.sum(e, axis=0, keepdims=True))
-            prob_bf = prob.astype(BF16)
-            ctx_t.append(dot_t(v_t[:, :keys], prob_bf, ((1,), (0,))).astype(BF16))
-            d_prob = dot_t(v[:keys], d_ctx[rows], ((1,), (1,)))
-            d_score = (prob * (d_prob - jnp.sum(d_prob * prob, axis=0, keepdims=True)) * scale).astype(BF16)
-            dq_t.append(dot_t(k_t[:, :keys], d_score, ((1,), (0,))))
-            dk.append(dot_t(d_score, q[rows], ((1,), (0,))))
-            dv.append(dot_t(prob_bf, d_ctx[rows], ((1,), (0,))))
-        ctx = jnp.concatenate(ctx_t, axis=1).T
-        ctx_ref[0, :, own] = ctx
-        ctx_all_ref[:, own] = ctx
-        d_q = rope(jnp.concatenate(dq_t, axis=1).T, -sin_t)
-        d_k = rope(jnp.concatenate([dk[0] + dk[1][:half], dk[1][half:]], axis=0), -sin_t)
-        d_v = jnp.concatenate([dv[0] + dv[1][:half], dv[1][half:]], axis=0)
+        loaded[i] = (q, k, v, dctx_ref[0, :, cols[0]], k.T, v.T)
+
+    def score(i, b):
+        if b == 0:
+            load_head(i)
+        q, k, v, d_ctx, _, _ = loaded[i]
+        rows, keys = slice(b * half, (b + 1) * half), (b + 1) * half
+        scored[i, b] = (dot_t(k[:keys], q[rows], ((1,), (1,))), dot_t(v[:keys], d_ctx[rows], ((1,), (1,))))
+
+    def softmax(i, b):
+        s, d_prob = scored.pop((i, b))
+        diag = jnp.where(mask, s[b * half:], -1e30)
+        s = diag if b == 0 else jnp.concatenate([s[:half], diag], axis=0)
+        e = jnp.exp2((s - jnp.max(s, axis=0, keepdims=True)) * (scale * LOG2E))
+        prob = e * (1.0 / jnp.sum(e, axis=0, keepdims=True))
+        d_score = (prob * (d_prob - jnp.sum(d_prob * prob, axis=0, keepdims=True)) * scale).astype(BF16)
+        soft[i, b] = (prob.astype(BF16), d_score)
+
+    def products(i, b):
+        prob_bf, d_score = soft.pop((i, b))
+        q, k, v, d_ctx, k_t, v_t = loaded[i]
+        rows, keys = slice(b * half, (b + 1) * half), (b + 1) * half
+        acc[b] = (dot_t(v_t[:, :keys], prob_bf, ((1,), (0,))).astype(BF16), dot_t(k_t[:, :keys], d_score, ((1,), (0,))),
+                  dot_t(d_score, q[rows], ((1,), (0,))), dot_t(prob_bf, d_ctx[rows], ((1,), (0,))))
+        if b == 0:
+            return
+        cols = head_cols(i)
+        ctx = jnp.concatenate([acc[0][0], acc[1][0]], axis=1).T
+        ctx_ref[0, :, cols[0]] = ctx
+        ctx_all_ref[:, cols[0]] = ctx
+        d_q = rope(jnp.concatenate([acc[0][1], acc[1][1]], axis=1).T, -sin_t)
+        d_k = rope(jnp.concatenate([acc[0][2] + acc[1][2][:half], acc[1][2][half:]], axis=0), -sin_t)
+        d_v = jnp.concatenate([acc[0][3] + acc[1][3][:half], acc[1][3][half:]], axis=0)
         for d_p, col in zip((d_q, d_k, d_v), cols):
             dqkv_ref[0, :, col] = d_p.astype(BF16)
             dqkv_all_ref[:, col] = d_p.astype(BF16)
             bsum_ref[:, col] += jnp.sum(d_p, axis=0, keepdims=True)
+
+    for n in range(len(units) + 2):
+        if n < len(units):
+            score(*units[n])
+        if 1 <= n <= len(units):
+            softmax(*units[n - 1])
+        if n >= 2:
+            products(*units[n - 2])
 
 
 def attention(qkv, d_ctx, cos_full, sin_full, heads, head_dim, half_rot, seq0, total, full):
@@ -141,11 +163,24 @@
 
 
 def front_h_kernel(tile, h_ref, wqkv_ref, bqkv_ref, wup_ref, bup_ref, qkv_ref, act_ref, slope_ref, act_all_ref, h_all_ref):
-    h = h_ref[...]
-    h_all_ref[...] = h
-    for j in range(act_ref.shape[1] // tile):
-        cols = slice(j * tile, (j + 1) * tile)
-        t = jnp.dot(h, wup_ref[:, cols], preferred_element_type=F32) + bup_ref[:, cols]
+    h_all_ref[...] = h_ref[...]
+    n_up, n_qkv = act_ref.shape[1], qkv_ref.shape[1]
+    jobs = []
+    ups = [('u', slice(j, j + tile)) for j in range(0, n_up, tile)]
+    qs = [('q', slice(j, min(j + tile, n_qkv))) for j in range(0, n_qkv, tile)]
+    while ups or qs:
+        jobs += [rest.pop(0) for rest in (ups, qs) if rest]
+
+    def product(kind, cols):
+        if kind == 'u':
+            return jnp.dot(h_ref[...], wup_ref[:, cols], preferred_element_type=F32)
+        return dot_t(h_ref[...], wqkv_ref[cols, :], ((1,), (1,)))
+
+    def finish(kind, cols, t):
+        if kind == 'q':
+            qkv_ref[:, cols] = (t + bqkv_ref[:, cols]).astype(BF16)
+            return
+        t = t + bup_ref[:, cols]
         t2 = t * t
         th = jnp.tanh(t * (GELU_A + (GELU_A * GELU_B) * t2))
         half_t = 0.5 * t
@@ -153,19 +188,23 @@
         act_ref[:, cols] = act
         act_all_ref[:, cols] = act
         slope_ref[:, cols] = 0.5 + 0.5 * th + half_t * (1.0 - th * th) * (GELU_A + (3 * GELU_A * GELU_B) * t2)
-    n = qkv_ref.shape[1]
-    for j in range(0, n, tile):
-        cols = slice(j, min(j + tile, n))
-        qkv_ref[:, cols] = (jnp.dot(h, wqkv_ref[:, cols], preferred_element_type=F32) + bqkv_ref[:, cols]).astype(BF16)
-
-
-def front_h(h, w_qkv, b_qkv, w_up, b_up, row0, total, full, bm=512, tile=256):
+
+    prev = None
+    for job in jobs:
+        t = product(*job)
+        if prev is not None:
+            finish(*prev)
+        prev = (*job, t)
+    finish(*prev)
+
+
+def front_h(h, w_qkv_t, b_qkv, w_up, b_up, row0, total, full, bm=256, tile=256):
     rows, d = h.shape
-    n1, n2 = w_qkv.shape[1], w_up.shape[1]
+    n1, n2 = w_qkv_t.shape[0], w_up.shape[1]
     blk = lambda c: pl.BlockSpec((bm, c), lambda i: (i, 0))
     off = lambda c: pl.BlockSpec((bm, c), lambda i: (i + row0 // bm, 0))
     return call(functools.partial(front_h_kernel, tile), "front_h", (rows // bm,),
-                [(h, blk(d)), const(w_qkv), const(b_qkv), const(w_up), const(b_up)],
+                [(h, blk(d)), const(w_qkv_t), const(b_qkv), const(w_up), const(b_up)],
                 [((rows, n1), BF16, blk(n1)), ((rows, n2), BF16, blk(n2)), ((rows, n2), F32, blk(n2)),
                  ((total, n2), BF16, off(n2)), ((total, d), BF16, off(d))], 2 * rows * d * (n1 + n2), full)
 
@@ -198,20 +237,31 @@
                  ((total, n2), BF16, off(n2)), ((total, d), BF16, off(d))], 2 * rows * d * (n1 + n2), full)
 
 
-def pair_kernel(tile, a_ref, b_ref, wa_ref, wb_ref, out_ref):
+def pair_kernel(tile, b_dim, a_ref, b_ref, wa_ref, wb_ref, out_ref):
     for j in range(out_ref.shape[1] // tile):
         cols = slice(j * tile, (j + 1) * tile)
+        wb = wb_ref[:, cols] if b_dim == 0 else wb_ref[cols, :]
         out_ref[:, cols] = (jnp.dot(a_ref[...], wa_ref[:, cols], preferred_element_type=F32)
-                            + jnp.dot(b_ref[...], wb_ref[:, cols], preferred_element_type=F32)).astype(BF16)
-
-
-def pair_matmul(a, b, wa, wb, name, bm=512, tile=256):
+                            + dot_t(b_ref[...], wb, ((1,), (b_dim,)))).astype(BF16)
+
+
+def pair_matmul(a, b, wa, wb, name, b_dim=0, bm=512, tile=256, splits=2):
     rows, ka = a.shape
-    kb, n = wb.shape
-    blk = lambda c: pl.BlockSpec((bm, c), lambda i: (i, 0))
-    return call(functools.partial(pair_kernel, tile), name, (rows // bm,),
-                [(a, blk(ka)), (b, blk(kb)), const(wa), const(wb)], [((rows, n), BF16, blk(n))],
-                2 * rows * (ka + kb) * n)[0]
+    kb, n = b.shape[1], wa.shape[1]
+    bn = n // splits
+    lhs = lambda c: pl.BlockSpec((bm, c), lambda j, i: (i, 0))
+    wb_spec = pl.BlockSpec((kb, bn), lambda j, i: (0, j)) if b_dim == 0 else pl.BlockSpec((bn, kb), lambda j, i: (j, 0))
+    return call(functools.partial(pair_kernel, tile, b_dim), name, (splits, rows // bm),
+                [(a, lhs(ka)), (b, lhs(kb)), (wa, pl.BlockSpec((ka, bn), lambda j, i: (0, j))), (wb, wb_spec)],
+                [((rows, n), BF16, pl.BlockSpec((bm, bn), lambda j, i: (i, j)))], 2 * rows * (ka + kb) * n)[0]
+
+
+def sum_over_tp(t):
+    n, step = lax.axis_size('tp'), 1
+    while step < n:
+        t = t + lax.ppermute(t, 'tp', [(i, i ^ step) for i in range(n)])
+        step *= 2
+    return t
 
 
 def layer_body(x_blk, rope_angle, ln_gain, ln_bias, w_q, b_q, w_k, b_k, w_v, b_v, w_o, b_o, w_up, b_up, w_down, b_down, dy_blk):
@@ -224,9 +274,8 @@
     pad = head_dim - 2 * half_rot
     cos_full = jnp.concatenate([jnp.cos(rope_angle)] * 2 + [jnp.ones((seq_len, pad), F32)], axis=-1)
     sin_full = jnp.concatenate([jnp.sin(rope_angle)] * 2 + [jnp.zeros((seq_len, pad), F32)], axis=-1)
-    w_qkv = jnp.concatenate([w_q, w_k, w_v], axis=1)
+    w_qkv_t = jnp.concatenate([w_q.T, w_k.T, w_v.T], axis=0)
     b_qkv = jnp.concatenate([b_q.reshape(1, -1), b_k.reshape(1, -1), b_v.reshape(1, -1)], axis=1)
-    w_qkv_t, w_up_t = w_qkv.T, w_up.T
 
     edges = [0]
     for part in CHUNK_PARTS:
@@ -252,7 +301,7 @@
         h, dy = h_full[c].reshape(rows, model_dim), dy_full[c].reshape(rows, model_dim)
         if tie is not None:
             h, tie = lax.optimization_barrier((h, tie))
-        qkv, act, slope, act_all, h_all = front_h(h, w_qkv, b_qkv, w_up, b_up.reshape(1, -1), row0, total, (act_all, h_all))
+        qkv, act, slope, act_all, h_all = front_h(h, w_qkv_t, b_qkv, w_up, b_up.reshape(1, -1), row0, total, (act_all, h_all))
         d_ctx, d_pre, b_part, dpre_all, dy_all = front_d(dy, w_o, w_down, slope, row0, total, (dpre_all, dy_all))
         bup_sum += b_part[0]
         ctx, d_qkv, b_part, ctx_all, dqkv_all = attention(
@@ -262,7 +311,7 @@
         ctx, d_qkv = ctx.reshape(rows, width), d_qkv.reshape(rows, 3 * width)
         branch = pair_matmul(ctx, act, w_o, w_down, "branch")
         d_qkv, branch = lax.optimization_barrier((d_qkv, branch))
-        d_h = pair_matmul(d_qkv, d_pre, w_qkv_t, w_up_t, "d_h")
+        d_h = pair_matmul(d_qkv, d_pre, w_qkv_t, w_up, "d_h", b_dim=1)
         tie = d_h
         branch_sum = lax.psum_scatter(branch.reshape(per, seq_len, model_dim), 'tp', scatter_dimension=1, tiled=True)
         y_all = call(residual_kernel, "residual", (per,), [(x_blk, row3(sl.start)), (branch_sum, row3()), const(bo), const(bdown)],
@@ -280,7 +329,7 @@
     g_down = dot_t(act_all, dy_all, t0)
     g_qkv = dot_t(h_all, dqkv_all, t0)
     g_up = dot_t(h_all, dpre_all, t0)
-    small = lax.psum(small, 'tp')
+    small = sum_over_tp(small)
     bsum = bsum.reshape(3, heads, head_dim)
     return (y_all, dx_all, small[0], small[1],
             g_qkv[:, :width], bsum[0], g_qkv[:, width:2 * width], bsum[1], g_qkv[:, 2 * width:], bsum[2],

time: 1020 us -> 945 us (0.926)
  Pallas kernels: 678 us -> 642 us
  blocking collectives: 24.7 us -> 0 us
  local copies, waits for them, and re-layouts: 47.5 us -> 29 us
    pallas_call x32 -> x24, Pallas kernels: 678 us -> 642 us  [call(): pl.pallas_call(body, grid=grid, in_specs=specs, out_specs=[s for _, _, s...]
    psum x1 -> x0, blocking collectives: 24.7 us -> none  [layer_body(): small = lax.psum(small, 'tp')]
    unnamed x52 -> x37, local copies, waits for them, and re-layouts: 14.1 us -> 1.32 us
    all_gather x4 -> x3, waiting for transfers between devices: 20.8 us -> 17.4 us  [layer_body(): dy_full.append(lax.all_gather(dy_blk[sl], 'tp', axis=1, tiled=True))]
  transfers between devices with their start and end apart: 16 -> 15, of which waited for: 2 -> 5; matrix products, arithmetic and copies ran while one was open for 24% -> 25% of each run, Pallas kernels for 64% -> 67%
where the time goes in v2:
time: 945 us; the launch traced here: 937 us
  Pallas kernels  642 us (68%)
  matrix products  202 us (21%)
  waiting for transfers between devices  37 us (4%)
  local copies, waits for them, and re-layouts  29 us (3%)
  between operations  14.7 us (2%)
    pallas_call x24, Pallas kernels, call(): pl.pallas_call(body, grid=grid, in_specs=specs, out_specs=[s for _, _, s...  642 us
    dot_general x4, matrix products, dot_t(): return lax.dot_general(a, b, (dims, ((), ())), preferred_element_type=F32)  202 us
  transfers between devices with their start and end apart: 15, of which 5 were waited for; matrix products, arithmetic and copies ran while one was open for 25% of the time, Pallas kernels for 67%

profile of v2, /device:TPU:112, one launch (start us, length us, event | category | flops | bytes accessed | tf_op | source)
XLA Modules:
  0.0 937.1 jit_solution(13758693316032359646)
XLA Ops:
  7.3 1.3 reshape.156.refs_1_.refs_3_
  8.6 1.3 reshape.157.refs_2_
  9.9 3.4 ln_fwd.5
  13.5 2.2 slice.61
  15.8 4.9 ln_fwd.4
  20.9 2.8 slice.62
  23.9 7.1 ln_fwd.3
  31.1 3.4 slice.63
  34.7 0.6 pad.2.clone
  35.3 0.1 reshape.161
  35.4 0.1 reshape.162
  35.5 0.1 reshape.163
  35.6 0.6 reshape.164.refs_4_
  36.2 0.8 fusion.1
  36.9 0.9 copy.53
  37.8 1.6 copy.51
  39.4 0.7 pad_maximum_fusion.1.refs_2_
  40.1 2.1 maximum_maximum_fusion
  42.2 3.5 pad_maximum_fusion.refs_1_.refs_2_
  45.7 13.9 %all-gather.11.cloned.1.call-done = bf16[3,512,2560]{2,1,0:T(8,128)(2,1)} async-done(((bf16[3,64,2560]{2,1,0:T(8,128)(2,1)}), bf16[3,512,2560]{2,1,0:T(8,128)(2,1)}) %all-gather.11.cloned.1.call-update) | async-done | bytes 7864336 | tf_op jit(solution)/shard_map/all_gather | solution.py:291
  59.6 28.3 %front_h.3 = (bf16[1536,960]{1,0:T(8,128)(2,1)}, bf16[1536,1280]{1,0:T(8,128)(2,1)}, f32[1536,1280]{1,0:T(8,128)}, bf16[8192,1280]{1,0:T(8,128)(2,1)}, bf16[8192,2560]{1,0:T(8,128)(2,1)}) custom-call(bf16[1536,2560]{1,0:T(8,128)(2,1)} %bitcast.48, bf16[960,2560]{1,0:T(8,128)(2,1)} %pad_maximum_fusion.refs_1_.refs_2_, f32[1,960]{1,0:T(1,128)} %pad_maximum_fusion.1.refs_2_, ...), custom_call_target="tpu_custom_call" | custom-call | flops 17616076800 | bytes 19342080 | tf_op jit(solution)/shard_map/front_h/pallas_call | solution.py:36
  87.9 17.4 %all-gather.13.cloned.1.call-done = bf16[3,512,2560]{2,1,0:T(8,128)(2,1)} async-done(((bf16[3,64,2560]{2,1,0:T(8,128)(2,1)}), bf16[3,512,2560]{2,1,0:T(8,128)(2,1)}) %all-gather.13.cloned.1.call-update) | async-done | bytes 7864336 | tf_op jit(solution)/shard_map/all_gather | solution.py:292
  105.2 20.9 %front_d.3 = (bf16[1536,320]{1,0:T(8,128)(2,1)}, bf16[1536,1280]{1,0:T(8,128)(2,1)}, f32[1,1280]{1,0:T(1,128)}, bf16[8192,1280]{1,0:T(8,128)(2,1)}, bf16[8192,2560]{1,0:T(8,128)(2,1)}) custom-call(bf16[1536,2560]{1,0:T(8,128)(2,1)} %bitcast.49, bf16[320,2560]{1,0:T(8,128)(2,1)} %refs_2_.11, bf16[1280,2560]{1,0:T(8,128)(2,1)} %refs_3_.16, ...), custom_call_target="tpu_custom_call" | custom-call | flops 12582912000 | bytes 23920640 | tf_op jit(solution)/shard_map/front_d/pallas_call | solution.py:36
  126.1 27.5 %attention.3 = (bf16[3,512,320]{2,1,0:T(8,128)(2,1)}, bf16[3,512,960]{2,1,0:T(8,128)(2,1)}, f32[1,960]{1,0:T(1,128)}, bf16[8192,320]{1,0:T(8,128)(2,1)}, bf16[8192,960]{1,0:T(8,128)(2,1)}) custom-call(bf16[3,512,960]{2,1,0:T(8,128)(2,1)} %bitcast.55, bf16[3,512,320]{2,1,0:T(8,128)(2,1)} %bitcast.60, f32[512,80]{1,0:T(8,128)} %get-tuple-element.165.refs_2_, ...), custom_call_target="tpu_custom_call" | custom-call | flops 6442450944 | bytes 4259840 | tf_op jit(solution)/shard_map/attention/pallas_call | solution.py:36
  153.6 19.8 %branch.3 = bf16[1536,2560]{1,0:T(8,128)(2,1)} custom-call(bf16[1536,320]{1,0:T(8,128)(2,1)} %bitcast.61, bf16[1536,1280]{1,0:T(8,128)(2,1)} %get-tuple-element.90.refs_1_, bf16[320,2560]{1,0:T(8,128)(2,1)} %refs_2_.11, bf16[1280,2560]{1,0:T(8,128)(2,1)} %refs_3_.16), custom_call_target="tpu_custom_call" | custom-call | flops 12582912000 | bytes 13107200 | tf_op jit(solution)/shard_map/branch/pallas_call | solution.py:36
  173.6 24.8 %d_h.3 = bf16[1536,2560]{1,0:T(8,128)(2,1)} custom-call(bf16[1536,960]{1,0:T(8,128)(2,1)} %bitcast.56, bf16[1536,1280]{1,0:T(8,128)(2,1)} %get-tuple-element.92.refs_1_, bf16[960,2560]{1,0:T(8,128)(2,1)} %pad_maximum_fusion.refs_1_.refs_2_, bf16[2560,1280]{1,0:T(8,128)(2,1)} %refs_3_.17), custom_call_target="tpu_custom_call" | custom-call | flops 17616076800 | bytes 18350080 | tf_op jit(solution)/shard_map/d_h/pallas_call | solution.py:36
  198.5 42.9 %front_h.4 = (bf16[2560,960]{1,0:T(8,128)(2,1)}, bf16[2560,1280]{1,0:T(8,128)(2,1)}, f32[2560,1280]{1,0:T(8,128)}, bf16[8192,1280]{1,0:T(8,128)(2,1)}, bf16[8192,2560]{1,0:T(8,128)(2,1)}) custom-call(bf16[2560,2560]{1,0:T(8,128)(2,1)} %bitcast.47, bf16[960,2560]{1,0:T(8,128)(2,1)} %pad_maximum_fusion.refs_1_.refs_2_, ...), custom_call_target="tpu_custom_call", output_to_operand_aliasing={{3}: (5, {}), {4}: (6, {})} | custom-call | flops 29360128000 | bytes 24584960 | tf_op jit(solution)/shard_map/front_h/pallas_call | solution.py:36
  241.4 30.9 %front_d.4 = (bf16[2560,320]{1,0:T(8,128)(2,1)}, bf16[2560,1280]{1,0:T(8,128)(2,1)}, f32[1,1280]{1,0:T(1,128)}, bf16[8192,1280]{1,0:T(8,128)(2,1)}, bf16[8192,2560]{1,0:T(8,128)(2,1)}) custom-call(bf16[2560,2560]{1,0:T(8,128)(2,1)} %bitcast.39, bf16[320,2560]{1,0:T(8,128)(2,1)} %refs_2_.11, ...), custom_call_target="tpu_custom_call", output_to_operand_aliasing={{3}: (4, {}), {4}: (5, {})} | custom-call | flops 20971520000 | bytes 34406400 | tf_op jit(solution)/shard_map/front_d/pallas_call | solution.py:36
  272.4 43.7 %attention.4 = (bf16[5,512,320]{2,1,0:T(8,128)(2,1)}, bf16[5,512,960]{2,1,0:T(8,128)(2,1)}, f32[1,960]{1,0:T(1,128)}, bf16[8192,320]{1,0:T(8,128)(2,1)}, bf16[8192,960]{1,0:T(8,128)(2,1)}) custom-call(bf16[5,512,960]{2,1,0:T(8,128)(2,1)} %bitcast.53, bf16[5,512,320]{2,1,0:T(8,128)(2,1)} %bitcast.50, ...), custom_call_target="tpu_custom_call", output_to_operand_aliasing={{3}: (4, {}), {4}: (5, {})} | custom-call | flops 10737418240 | bytes 6881280 | tf_op jit(solution)/shard_map/attention/pallas_call | solution.py:36
  316.1 30.1 %branch.4 = bf16[2560,2560]{1,0:T(8,128)(2,1)} custom-call(bf16[2560,320]{1,0:T(8,128)(2,1)} %bitcast.59, bf16[2560,1280]{1,0:T(8,128)(2,1)} %get-tuple-element.105.refs_1_, bf16[320,2560]{1,0:T(8,128)(2,1)} %refs_2_.11, bf16[1280,2560]{1,0:T(8,128)(2,1)} %refs_3_.16), custom_call_target="tpu_custom_call" | custom-call | flops 20971520000 | bytes 16384000 | tf_op jit(solution)/shard_map/branch/pallas_call | solution.py:36
  346.4 37.9 %d_h.4 = bf16[2560,2560]{1,0:T(8,128)(2,1)} custom-call(bf16[2560,960]{1,0:T(8,128)(2,1)} %bitcast.54, bf16[2560,1280]{1,0:T(8,128)(2,1)} %get-tuple-element.107.refs_1_, bf16[960,2560]{1,0:T(8,128)(2,1)} %pad_maximum_fusion.refs_1_.refs_2_, bf16[2560,1280]{1,0:T(8,128)(2,1)} %refs_3_.17), custom_call_target="tpu_custom_call" | custom-call | flops 29360128000 | bytes 22937600 | tf_op jit(solution)/shard_map/d_h/pallas_call | solution.py:36
  384.5 64.7 %front_h.5 = (bf16[4096,960]{1,0:T(8,128)(2,1)}, bf16[4096,1280]{1,0:T(8,128)(2,1)}, f32[4096,1280]{1,0:T(8,128)}, bf16[8192,1280]{1,0:T(8,128)(2,1)}, bf16[8192,2560]{1,0:T(8,128)(2,1)}) custom-call(bf16[4096,2560]{1,0:T(8,128)(2,1)} %bitcast.46, bf16[960,2560]{1,0:T(8,128)(2,1)} %pad_maximum_fusion.refs_1_.refs_2_, ...), custom_call_target="tpu_custom_call", output_to_operand_aliasing={{3}: (5, {}), {4}: (6, {})} | custom-call | flops 46976204800 | bytes 32449280 | tf_op jit(solution)/shard_map/front_h/pallas_call | solution.py:36
  449.2 45.9 %front_d.5 = (bf16[4096,320]{1,0:T(8,128)(2,1)}, bf16[4096,1280]{1,0:T(8,128)(2,1)}, f32[1,1280]{1,0:T(1,128)}, bf16[8192,1280]{1,0:T(8,128)(2,1)}, bf16[8192,2560]{1,0:T(8,128)(2,1)}) custom-call(bf16[4096,2560]{1,0:T(8,128)(2,1)} %bitcast.45, bf16[320,2560]{1,0:T(8,128)(2,1)} %refs_2_.11, ...), custom_call_target="tpu_custom_call", output_to_operand_aliasing={{3}: (4, {}), {4}: (5, {})} | custom-call | flops 33554432000 | bytes 50135040 | tf_op jit(solution)/shard_map/front_d/pallas_call | solution.py:36
  495.1 68.4 %attention.5 = (bf16[8,512,320]{2,1,0:T(8,128)(2,1)}, bf16[8,512,960]{2,1,0:T(8,128)(2,1)}, f32[1,960]{1,0:T(1,128)}, bf16[8192,320]{1,0:T(8,128)(2,1)}, bf16[8192,960]{1,0:T(8,128)(2,1)}) custom-call(bf16[8,512,960]{2,1,0:T(8,128)(2,1)} %bitcast.51, bf16[8,512,320]{2,1,0:T(8,128)(2,1)} %bitcast.57, ...), custom_call_target="tpu_custom_call", output_to_operand_aliasing={{3}: (4, {}), {4}: (5, {})} | custom-call | flops 17179869184 | bytes 10813440 | tf_op jit(solution)/shard_map/attention/pallas_call | solution.py:36
  563.4 45.6 %branch.5 = bf16[4096,2560]{1,0:T(8,128)(2,1)} custom-call(bf16[4096,320]{1,0:T(8,128)(2,1)} %bitcast.58, bf16[4096,1280]{1,0:T(8,128)(2,1)} %get-tuple-element.120.refs_1_, bf16[320,2560]{1,0:T(8,128)(2,1)} %refs_2_.11, bf16[1280,2560]{1,0:T(8,128)(2,1)} %refs_3_.16), custom_call_target="tpu_custom_call" | custom-call | flops 33554432000 | bytes 21299200 | tf_op jit(solution)/shard_map/branch/pallas_call | solution.py:36
  609.2 57.6 %d_h.5 = bf16[4096,2560]{1,0:T(8,128)(2,1)} custom-call(bf16[4096,960]{1,0:T(8,128)(2,1)} %bitcast.52, bf16[4096,1280]{1,0:T(8,128)(2,1)} %get-tuple-element.122.refs_1_, bf16[960,2560]{1,0:T(8,128)(2,1)} %pad_maximum_fusion.refs_1_.refs_2_, bf16[2560,1280]{1,0:T(8,128)(2,1)} %refs_3_.17), custom_call_target="tpu_custom_call" | custom-call | flops 46976204800 | bytes 29818880 | tf_op jit(solution)/shard_map/d_h/pallas_call | solution.py:36
  666.9 0.6 copy-done.6
  667.5 0.6 reshape.182.refs_2_
  668.2 0.6 reshape.183.refs_3_
  668.8 3.4 residual.3.refs_4_
  672.2 5.1 ln_bwd.3
  677.2 51.2 %fusion.2 = f32[2560,960]{0,1:T(8,128)} fusion(bf16[8192,2560]{1,0:T(8,128)(2,1)} %get-tuple-element.142, bf16[8192,960]{1,0:T(8,128)(2,1)} %get-tuple-element.143), kind=kOutput, calls=%fused_computation.15 | convolution fusion | flops 40265318400 | bytes 67502080 | tf_op jit(solution)/shard_map/dot_general | solution.py:18
  728.4 7.9 fusion
  736.3 24.1 %fusion.3 = f32[320,2560]{1,0:T(8,128)} fusion(bf16[8192,320]{1,0:T(8,128)(2,1)} %get-tuple-element.147, bf16[8192,2560]{1,0:T(8,128)(2,1)} %get-tuple-element.148), kind=kOutput, calls=%fused_computation.16 | convolution fusion | flops 13421772800 | bytes 50462720 | tf_op jit(solution)/shard_map/dot_general | solution.py:18
  760.4 63.3 %fusion.4 = f32[2560,1280]{1,0:T(8,128)} fusion(bf16[8192,2560]{1,0:T(8,128)(2,1)} %get-tuple-element.142, bf16[8192,1280]{1,0:T(8,128)(2,1)} %get-tuple-element.149), kind=kOutput, calls=%fused_computation.17 | convolution fusion | flops 53687091200 | bytes 76021760 | tf_op jit(solution)/shard_map/dot_general | solution.py:18
  823.8 63.5 %fusion.5 = f32[1280,2560]{1,0:T(8,128)} fusion(bf16[8192,1280]{1,0:T(8,128)(2,1)} %get-tuple-element.153, bf16[8192,2560]{1,0:T(8,128)(2,1)} %get-tuple-element.148), kind=kOutput, calls=%fused_computation.18 | convolution fusion | flops 53687091200 | bytes 76021760 | tf_op jit(solution)/shard_map/dot_general | solution.py:18
  887.3 4.8 residual.4.refs_4_
  892.1 7.3 ln_bwd.4
  899.4 6.7 residual.5
  906.2 10.6 %ln_bwd.5 = (f32[8,2560]{1,0:T(8,128)}, f32[16,64,2560]{2,1,0:T(8,128)}) custom-call(bf16[16,64,2560]{2,1,0:T(8,128)(2,1)} %refs_0_.17, bf16[16,64,2560]{2,1,0:T(8,128)(2,1)} %refs_1_.11, bf16[8,64,2560]{2,1,0:T(8,128)(2,1)} %reduce-scatter.7.cloned.1.call-done.refs_2_, f32[1,2560]{1,0:T(1,128)} %reshape.156.refs_1_.refs_3_, ...), custom_call_target="tpu_custom_call", output_to_operand_aliasing={{1}: (4, {})} | custom-call | flops 262144000 | bytes 13117440 | tf_op jit(solution)/shard_map/ln_bwd/pallas_call | solution.py:36
  916.8 0.9 slice_add_fusion
  917.7 0.3 collective-permute-start
  918.1 0.9 collective-permute-done
  919.0 0.8 collective-permute-start.1
  919.9 0.6 add_reduce_fusion
  920.5 2.6 collective-permute-done.1
  923.1 2.0 collective-permute-start.2
  925.2 0.1 slice_reduce_fusion.3
  925.3 0.7 slice.77
  925.9 0.7 slice.74
  926.6 0.7 slice.71
  927.2 1.5 collective-permute-done.2
  928.7 0.7 slice_reduce_fusion
  929.4 0.6 copy.72
  (76 shorter events, 1.7 us)
Async XLA Ops:
  7.2 52.4 %all-gather.11.cloned.1.call-start = ((), (), s32[]{:S(2)}) async-start(), calls=%async_computation.8 | async-start | bytes 8847360 | tf_op jit(solution)/shard_map/all_gather | solution.py:291
  13.4 91.8 %all-gather.13.cloned.1.call-start = ((), (), s32[]{:S(2)}) async-start(), calls=%async_computation.9 | async-start | bytes 8847360 | tf_op jit(solution)/shard_map/all_gather | solution.py:292
  15.7 182.8 %all-gather.9.cloned.1.call-start = ((), (), s32[]{:S(2)}) async-start(), calls=%async_computation.7 | async-start | bytes 14745600 | tf_op jit(solution)/shard_map/all_gather | solution.py:291
  20.8 220.6 %all-gather.15.cloned.1.call-start = ((), (), s32[]{:S(2)}) async-start(), calls=%async_computation.10 | async-start | bytes 14745600 | tf_op jit(solution)/shard_map/all_gather | solution.py:292
  23.7 11.6 %copy-start.15 = (f32[4,80]{1,0:T(4,128)S(1)}, f32[4,80]{1,0:T(4,128)}, u32[]{:S(2)}) copy-start(f32[4,80]{1,0:T(4,128)} %param.22) | copy-start | bytes 3844
  23.7 11.7 %copy-start.16 = (f32[4,80]{1,0:T(4,128)S(1)}, f32[4,80]{1,0:T(4,128)}, u32[]{:S(2)}) copy-start(f32[4,80]{1,0:T(4,128)} %param.24) | copy-start | bytes 3844
  23.7 11.8 %copy-start.17 = (f32[4,80]{1,0:T(4,128)S(1)}, f32[4,80]{1,0:T(4,128)}, u32[]{:S(2)}) copy-start(f32[4,80]{1,0:T(4,128)} %param.26) | copy-start | bytes 3844
  23.7 11.9 %copy-start.8 = (f32[1280]{0:T(1024)S(1)}, f32[1280]{0:T(1024)}, u32[]{:S(2)}) copy-start(f32[1280]{0:T(1024)} %param.30) | copy-start | bytes 15364
  23.7 12.5 %copy-start.3 = (f32[512,16]{0,1:T(8,128)S(1)}, f32[512,16]{0,1:T(8,128)}, u32[]{:S(2)}) copy-start(f32[512,16]{0,1:T(8,128)} %param.18) | copy-start | bytes 98308
  23.8 18.4 %copy-start = (bf16[2560,320]{0,1:T(8,128)(2,1)S(1)}, bf16[2560,320]{0,1:T(8,128)(2,1)}, u32[]{:S(2)}) copy-start(bf16[2560,320]{0,1:T(8,128)(2,1)} %param.25) | copy-start | bytes 4915204
  23.8 18.4 %copy-start.1 = (bf16[2560,320]{0,1:T(8,128)(2,1)S(1)}, bf16[2560,320]{0,1:T(8,128)(2,1)}, u32[]{:S(2)}) copy-start(bf16[2560,320]{0,1:T(8,128)(2,1)} %param.23) | copy-start | bytes 4915204
  23.8 360.7 %all-gather.7.cloned.1.call-start = ((), (), s32[]{:S(2)}) async-start(), calls=%async_computation.6 | async-start | bytes 23592960 | tf_op jit(solution)/shard_map/all_gather | solution.py:291
  31.0 418.1 %all-gather.17.cloned.1.call-start = ((), (), s32[]{:S(2)}) async-start(), calls=%async_computation.11 | async-start | bytes 23592960 | tf_op jit(solution)/shard_map/all_gather | solution.py:292
  34.6 634.2 %reduce-scatter.17.cloned.1.call-start = ((), (), s32[]{:S(2)}) async-start(), calls=%async_computation.17 | async-start | bytes 8847360 | tf_op jit(solution)/shard_map/reduce_scatter | solution.py:316
  173.5 498.7 %reduce-scatter.15.cloned.1.call-start = ((), (), s32[]{:S(2)}) async-start(), calls=%async_computation.16 | async-start | bytes 8847360 | tf_op jit(solution)/shard_map/reduce_scatter | solution.py:319
  198.4 688.9 %reduce-scatter.13.cloned.1.call-start = ((), (), s32[]{:S(2)}) async-start(), calls=%async_computation.15 | async-start | bytes 14745600 | tf_op jit(solution)/shard_map/reduce_scatter | solution.py:316
  346.3 545.8 %reduce-scatter.11.cloned.1.call-start = ((), (), s32[]{:S(2)}) async-start(), calls=%async_computation.14 | async-start | bytes 14745600 | tf_op jit(solution)/shard_map/reduce_scatter | solution.py:319
  384.4 515.0 %reduce-scatter.9.cloned.1.call-start = ((), (), s32[]{:S(2)}) async-start(), calls=%async_computation.13 | async-start | bytes 23592960 | tf_op jit(solution)/shard_map/reduce_scatter | solution.py:316
  609.1 297.0 %reduce-scatter.7.cloned.1.call-start = ((), (), s32[]{:S(2)}) async-start(), calls=%async_computation.12 | async-start | bytes 23592960 | tf_op jit(solution)/shard_map/reduce_scatter | solution.py:319
  666.8 0.7 copy-start.6
  666.8 1.3 copy-start.7
  906.1 10.7 %copy-start.4 = (f32[8,2560]{1,0:T(8,128)S(1)}, f32[8,2560]{1,0:T(8,128)}, u32[]{:S(2)}) copy-start(f32[8,2560]{1,0:T(8,128)} %get-tuple-element.135) | copy-start | bytes 245764
  906.1 10.7 %copy-start.5 = (f32[8,2560]{1,0:T(8,128)S(1)}, f32[8,2560]{1,0:T(8,128)}, u32[]{:S(2)}) copy-start(f32[8,2560]{1,0:T(8,128)} %get-tuple-element.136) | copy-start | bytes 245764
  906.1 11.9 %copy-start.12 = (f32[1,960]{1,0:T(1,128)S(1)}, f32[1,960]{1,0:T(1,128)}, u32[]{:S(2)}) copy-start(f32[1,960]{1,0:T(1,128)} %get-tuple-element.144) | copy-start | bytes 11524
  906.2 11.9 %copy-start.13 = (f32[1,960]{1,0:T(1,128)S(1)}, f32[1,960]{1,0:T(1,128)}, u32[]{:S(2)}) copy-start(f32[1,960]{1,0:T(1,128)} %get-tuple-element.145) | copy-start | bytes 11524
  906.2 11.9 %copy-start.14 = (f32[1,960]{1,0:T(1,128)S(1)}, f32[1,960]{1,0:T(1,128)}, u32[]{:S(2)}) copy-start(f32[1,960]{1,0:T(1,128)} %get-tuple-element.146) | copy-start | bytes 11524
  906.2 13.7 %copy-start.9 = (f32[1,1280]{1,0:T(1,128)S(1)}, f32[1,1280]{1,0:T(1,128)}, u32[]{:S(2)}) copy-start(f32[1,1280]{1,0:T(1,128)} %get-tuple-element.150) | copy-start | bytes 15364
  906.2 13.7 %copy-start.10 = (f32[1,1280]{1,0:T(1,128)S(1)}, f32[1,1280]{1,0:T(1,128)}, u32[]{:S(2)}) copy-start(f32[1,1280]{1,0:T(1,128)} %get-tuple-element.151) | copy-start | bytes 15364
  906.2 13.7 %copy-start.11 = (f32[1,1280]{1,0:T(1,128)S(1)}, f32[1,1280]{1,0:T(1,128)}, u32[]{:S(2)}) copy-start(f32[1,1280]{1,0:T(1,128)} %get-tuple-element.152) | copy-start | bytes 15364
  917.7 1.3 collective-permute-start
  919.0 4.1 collective-permute-start.1
  923.1 5.6 collective-permute-start.2
  929.4 0.6 copy-start.2
Sparse Core Ops, SparseCore 0:
  13.5 46.0 all-gather.10
  61.8 43.4 all-gather.12
  107.4 65.6 all-gather.8
  174.5 65.8 all-gather.14
  242.4 99.3 all-gather.6
  343.9 99.6 all-gather.16
  445.8 46.6 reduce-scatter.16
  494.8 45.5 reduce-scatter.14
  542.7 70.5 reduce-scatter.12
  615.4 70.5 reduce-scatter.10
  688.3 107.2 reduce-scatter.8
  797.8 107.2 reduce-scatter.6
